TPU v7x, 32 devices: a whole 2x2x4 slice. The times are simulated.
32 devices in a mesh: types: 4 (over y, x), inst: 2 (over core), face: 4 (over z).
Axes of the slice: x: 2, y: 2, z: 4, core: 2. Of those that a mesh axis runs over, the one named last changes fastest.
Arguments:
- coupling_modes: bfloat16 [8, 1024, 16384], P(('types', 'inst'), None, 'face'), may hold values from -0.0625 to 0.0625
- mode_stiffness: float32 [8, 16384], P(('types', 'inst'), 'face'), may hold values from 1 to 8
- boundary_stiffness: float32 [8, 1024, 1024], P(('types', 'inst'), 'face'), may hold values from -1 to 9, as said below
- slot_type: int32 [4, 2, 4, 2], P('types', 'inst', 'face'), may hold values from 0 to 1
- partner_slot: int32 [4, 2, 4, 3, 2], P('types', 'inst', 'face'), may hold values from 0 to 1, each once within a row
- port_map: int32 [4, 2, 4, 3, 2, 128], P('types', 'inst', 'face'), may hold values from 0 to 127, each once within a row
- loads: float32 [4, 2, 4, 2, 1024, 128], P('types', 'inst', 'face'), may hold values from -24 to 24
Outputs:
- displacement: float32 [4, 2, 4, 2, 1024, 128], P('types', 'inst', 'face')
Inputs may be any that keep to these rules, and one draw needn't show every extreme that they name: `boundary_stiffness`: each type's matrix is symmetric.
All inputs are finite; a program needn't handle non-finite values.
Results may differ from a plain program's by a relative error of at most 0.004.
Values may be sent and summed in bfloat16 or wider, within the bound.
No kernel may reach another device: no remote copies, remote signals or barrier semaphores. Data moves between devices by JAX's collectives and lax.ppermute only.
A program may use at most 128 MiB of HBM per device.

v0:
```python
import jax
import jax.numpy as jnp
from jax import lax
from jax.sharding import PartitionSpec as P

SIDES = 8
SWEEPS = 4


lower_bound = 2.0
upper_bound = 12.0


def with_halo(block, sides, width):
    for axis, dim in sides:
        count = lax.axis_size(axis)
        forward = [(i, i + 1) for i in range(count - 1)]
        backward = [(target, source) for source, target in forward]
        low = lax.ppermute(
            lax.slice_in_dim(block, block.shape[dim] - width, None, axis=dim), axis, forward
        )
        high = lax.ppermute(lax.slice_in_dim(block, 0, width, axis=dim), axis, backward)
        block = jnp.concatenate([low, block, high], axis=dim)
    return block


def port_table(slot_ids, port_ids, slot_total, port_width):
    targets = (slot_ids[:, None] * port_width + port_ids).reshape(-1)
    columns = lax.broadcasted_iota(jnp.int32, (slot_total * port_width, slot_total * port_width), 1)
    return (columns == targets[:, None]).astype(jnp.float32)


def fetch_ports(source, matcher):
    slot_total, port_width, load_count = source.shape
    flat = jnp.dot(matcher, source.reshape(-1, load_count), precision=lax.Precision.HIGHEST)
    return flat.reshape(slot_total, port_width, load_count)


def place_ports(values, matcher):
    slot_total, port_width, load_count = values.shape
    flat = lax.dot_general(
        matcher,
        values.reshape(-1, load_count),
        (((0,), (0,)), ((), ())),
        precision=lax.Precision.HIGHEST,
    )
    return flat.reshape(slot_total, port_width, load_count)


def per_device(
    coupling_modes, mode_stiffness, boundary_stiffness, slot_type, partner_slot, port_map, loads
):
    scaled = (coupling_modes[0].astype(jnp.float32) / mode_stiffness[0][None, :]).astype(
        jnp.bfloat16
    )
    own_modes = coupling_modes[0]
    width = own_modes.shape[0]
    reduced = lax.psum_scatter(
        lax.dot_general(
            scaled, own_modes, (((1,), (1,)), ((), ())), preferred_element_type=jnp.float32
        ),
        "face",
        scatter_dimension=0,
        tiled=True,
    )
    blocks = (boundary_stiffness[0] - reduced).astype(jnp.bfloat16)
    stacked_rows = lax.all_gather(blocks, ("inst", "face"), axis=0, tiled=True)
    gathered = stacked_rows.reshape(-1, width, width)
    rhs = loads[0, 0, 0]
    slot_kinds = slot_type[0, 0, 0]
    partners = partner_slot[0, 0, 0]
    port_maps = port_map[0, 0, 0]
    slot_total = rhs.shape[0]
    load_count = rhs.shape[2]
    port_width = width // SIDES
    matrices = [
        lax.dynamic_index_in_dim(gathered, slot_kinds[number], 0, keepdims=False)
        for number in range(slot_total)
    ]
    matchers = [
        port_table(partners[number], port_maps[number], slot_total, port_width)
        for number in range(3)
    ]
    next_inst = (lax.axis_index("inst") < lax.axis_size("inst") - 1).astype(jnp.float32)
    prev_inst = (lax.axis_index("inst") > 0).astype(jnp.float32)
    next_face = (lax.axis_index("face") < lax.axis_size("face") - 1).astype(jnp.float32)
    prev_face = (lax.axis_index("face") > 0).astype(jnp.float32)
    next_types = (lax.axis_index("types") < lax.axis_size("types") - 1).astype(jnp.float32)
    prev_types = (lax.axis_index("types") > 0).astype(jnp.float32)

    def split_sides(values, direction):
        upper_side = values[:, 2 * direction * port_width : (2 * direction + 1) * port_width]
        lower_side = values[:, (2 * direction + 1) * port_width : (2 * direction + 2) * port_width]
        outgoing = place_ports(upper_side, matchers[direction])
        return (upper_side, lower_side, jnp.stack([lower_side, outgoing]))

    def side_terms(upper_side, lower_side, extended, direction, has_next, has_prev):
        partner = fetch_ports(extended[3], matchers[direction])
        return [has_next * (upper_side - partner), has_prev * (lower_side - extended[0])]

    def couple(values):
        upper_side, lower_side, stacked = split_sides(values, 0)
        extended = with_halo(stacked.astype(jnp.bfloat16), (("inst", 0),), 1).astype(stacked.dtype)
        terms = side_terms(upper_side, lower_side, extended, 0, next_inst, prev_inst)
        upper_side, lower_side, stacked = split_sides(values, 1)
        extended = with_halo(stacked.astype(jnp.bfloat16), (("face", 0),), 1).astype(stacked.dtype)
        terms = terms + side_terms(upper_side, lower_side, extended, 1, next_face, prev_face)
        upper_side, lower_side, stacked = split_sides(values, 2)
        extended = with_halo(stacked.astype(jnp.bfloat16), (("types", 0),), 1).astype(stacked.dtype)
        terms = terms + side_terms(upper_side, lower_side, extended, 2, next_types, prev_types)
        terms.append(jnp.zeros((slot_total, width - 6 * port_width, load_count), jnp.float32))
        return jnp.concatenate(terms, axis=1)

    def operator_apply(values):
        lowered = values.astype(jnp.bfloat16)
        product = jnp.stack(
            [
                jnp.dot(matrices[number], lowered[number], preferred_element_type=jnp.float32)
                for number in range(slot_total)
            ]
        )
        return product + couple(values)

    theta = (upper_bound + lower_bound) / 2.0
    delta = (upper_bound - lower_bound) / 2.0
    sigma = theta / delta
    weight_now = 1.0 / sigma
    displacement = jnp.zeros_like(rhs)
    residual = rhs
    direction = rhs / theta
    for sweep_index in range(SWEEPS):
        displacement = displacement + direction
        residual = residual - operator_apply(direction)
        weight_next = 1.0 / (2.0 * sigma - weight_now)
        direction = weight_next * weight_now * direction + 2.0 * weight_next / delta * residual
        weight_now = weight_next
    return displacement[None, None, None]


def solution(mesh):
    placed = (
        P(("types", "inst"), None, "face"),
        P(("types", "inst"), "face"),
        P(("types", "inst"), "face", None),
        P("types", "inst", "face", None),
        P("types", "inst", "face", None, None),
        P("types", "inst", "face", None, None, None),
        P("types", "inst", "face", None, None, None),
    )
    return jax.shard_map(
        per_device,
        mesh=mesh,
        in_specs=placed,
        out_specs=P("types", "inst", "face", None, None, None),
        check_vma=False,
    )
```

profile of v0, /device:TPU:12, one launch (start us, length us, event | category | flops | bytes accessed | tf_op | source)
XLA Modules:
  0.0 214.9 jit_solution(11437733609438386762)
XLA Ops:
  6.5 16.0 %fusion.1 = f32[1024,1024]{1,0:T(8,128)} fusion(bf16[1,1024,4096]{2,1,0:T(8,128)(2,1)} %param.7, f32[4096]{0:T(1024)} %bitcast.332), kind=kOutput, calls=%fused_computation.2 | convolution fusion | flops 8602517504 | bytes 12599296 | tf_op jit(solution)/shard_map/dot_general | solution.py:59
  22.6 78.0 %reduce-scatter.2.cloned.1.call-done = f32[256,1024]{1,0:T(8,128)} async-done(((f32[1024,1024]{1,0:T(8,128)}), f32[256,1024]{1,0:T(8,128)}) %reduce-scatter.2.cloned.1.call-update) | async-done | bytes 1048592 | tf_op jit(solution)/shard_map/reduce_scatter | solution.py:58
  100.6 2.2 %fusion.63 = bf16[256,1024]{1,0:T(8,128)(2,1)} fusion(f32[256,1024]{1,0:T(8,128)} %reduce-scatter.2.cloned.1.call-done, f32[1,256,1024]{2,1,0:T(8,128)S(1)} %copy-done.2), kind=kLoop, calls=%fused_computation.85 | loop fusion | flops 524288 | bytes 2621440 | tf_op jit(solution)/shard_map/convert_element_type | solution.py:66
  107.5 3.3 %collective-permute-start.4 = (bf16[1,2,128,128]{3,2,1,0:T(8,128)(2,1)}, bf16[1,2,128,128]{3,2,1,0:T(8,128)(2,1)S(1)}, u32[]{:S(2)}, u32[]{:S(2)}) collective-permute-start(bf16[1,2,128,128]{3,2,1,0:T(8,128)(2,1)} %get-tuple-element.29), channel_id=1, source_target_pairs={{8,0},{16,8},{24,16},{9,1},{17,9},{25,17},{10,2},{18,10},{26,18},{... | collective-permute-start | bytes 196616 | tf_op jit(solution)/shard_map/ppermute | solution.py:22
  110.8 2.2 %collective-permute-start.2 = (bf16[1,2,128,128]{3,2,1,0:T(8,128)(2,1)}, bf16[1,2,128,128]{3,2,1,0:T(8,128)(2,1)S(1)}, u32[]{:S(2)}, u32[]{:S(2)}) collective-permute-start(bf16[1,2,128,128]{3,2,1,0:T(8,128)(2,1)} %get-tuple-element.30), channel_id=1, source_target_pairs={{1,0},{2,1},{3,2},{5,4},{6,5},{7,6},{9,8},{10,9},{11,10},{13,12},{... | collective-permute-start | bytes 196616 | tf_op jit(solution)/shard_map/ppermute | solution.py:22
  122.2 3.6 %collective-permute-start.3 = (bf16[1,2,128,128]{3,2,1,0:T(8,128)(2,1)S(1)}, bf16[1,2,128,128]{3,2,1,0:T(8,128)(2,1)S(1)}, u32[]{:S(2)}, u32[]{:S(2)}) collective-permute-start(bf16[1,2,128,128]{3,2,1,0:T(8,128)(2,1)S(1)} %fusion.44), channel_id=1, source_target_pairs={{0,1},{1,2},{2,3},{4,5},{5,6},{6,7},{8,9},{9,10},{10,11},{12,13},{... | collective-permute-start | bytes 196616 | tf_op jit(solution)/shard_map/ppermute | solution.py:19
  128.0 2.5 %collective-permute-done.3 = bf16[1,2,128,128]{3,2,1,0:T(8,128)(2,1)S(1)} collective-permute-done((bf16[1,2,128,128]{3,2,1,0:T(8,128)(2,1)S(1)}, bf16[1,2,128,128]{3,2,1,0:T(8,128)(2,1)S(1)}, u32[]{:S(2)}, u32[]{:S(2)}) %collective-permute-start.3) | collective-permute-done | bytes 65568 | tf_op jit(solution)/shard_map/ppermute | solution.py:19
  130.9 2.5 %collective-permute-start.5 = (bf16[1,2,128,128]{3,2,1,0:T(8,128)(2,1)S(1)}, bf16[1,2,128,128]{3,2,1,0:T(8,128)(2,1)S(1)}, u32[]{:S(2)}, u32[]{:S(2)}) collective-permute-start(bf16[1,2,128,128]{3,2,1,0:T(8,128)(2,1)S(1)} %fusion.45), channel_id=1, source_target_pairs={{0,8},{8,16},{16,24},{1,9},{9,17},{17,25},{2,10},{10,18},{18,26},{... | collective-permute-start | bytes 196616 | tf_op jit(solution)/shard_map/ppermute | solution.py:19
  135.0 3.0 %collective-permute-done.5 = bf16[1,2,128,128]{3,2,1,0:T(8,128)(2,1)S(1)} collective-permute-done((bf16[1,2,128,128]{3,2,1,0:T(8,128)(2,1)S(1)}, bf16[1,2,128,128]{3,2,1,0:T(8,128)(2,1)S(1)}, u32[]{:S(2)}, u32[]{:S(2)}) %collective-permute-start.5) | collective-permute-done | bytes 65568 | tf_op jit(solution)/shard_map/ppermute | solution.py:19
  139.4 11.2 %all-gather.2.cloned.1.call-done = bf16[2048,1024]{1,0:T(8,128)(2,1)} async-done(((bf16[256,1024]{1,0:T(8,128)(2,1)}), bf16[2048,1024]{1,0:T(8,128)(2,1)}) %all-gather.2.cloned.1.call-update) | async-done | bytes 4194320 | tf_op jit(solution)/shard_map/all_gather | solution.py:67
  150.6 2.3 %fusion.8 = f32[1024,128]{1,0:T(8,128)S(1)} fusion(bf16[2,1024,1024]{2,1,0:T(8,128)(2,1)} %bitcast.289, s32[]{:T(128)S(6)} %select_n.8, bf16[2,1024,128]{2,1,0:T(8,128)(2,1)} %get-tuple-element.25), kind=kOutput, calls=%fused_computation.8 | convolution fusion | flops 268435456 | bytes 2883588 | tf_op jit(solution)/shard_map/dot_general | solution.py:118
  152.9 2.5 %fusion.14 = f32[1024,128]{1,0:T(8,128)S(1)} fusion(bf16[2,1024,1024]{2,1,0:T(8,128)(2,1)} %bitcast.290, s32[]{:T(128)S(6)} %select_n.7, bf16[2,1024,128]{2,1,0:T(8,128)(2,1)} %get-tuple-element.25), kind=kOutput, calls=%fused_computation.14 | convolution fusion | flops 268435456 | bytes 2883588 | tf_op jit(solution)/shard_map/dot_general | solution.py:118
  158.8 3.0 %collective-permute-start.7 = (bf16[1,2,128,128]{3,2,1,0:T(8,128)(2,1)S(1)}, bf16[1,2,128,128]{3,2,1,0:T(8,128)(2,1)S(1)}, u32[]{:S(2)}, u32[]{:S(2)}) collective-permute-start(bf16[1,2,128,128]{3,2,1,0:T(8,128)(2,1)S(1)} %fusion.46), channel_id=1, source_target_pairs={{0,4},{1,5},{2,6},{3,7},{8,12},{9,13},{10,14},{11,15},{16,20},{17,... | collective-permute-start | bytes 196616 | tf_op jit(solution)/shard_map/ppermute | solution.py:19
  161.8 3.3 %collective-permute-start.10 = (bf16[1,2,128,128]{3,2,1,0:T(8,128)(2,1)S(1)}, bf16[1,2,128,128]{3,2,1,0:T(8,128)(2,1)S(1)}, u32[]{:S(2)}, u32[]{:S(2)}) collective-permute-start(bf16[1,2,128,128]{3,2,1,0:T(8,128)(2,1)S(1)} %get-tuple-element.20), channel_id=1, source_target_pairs={{8,0},{16,8},{24,16},{9,1},{17,9},{25,17},{10,2},{18,10},{26,18},{... | collective-permute-start | bytes 196616 | tf_op jit(solution)/shard_map/ppermute | solution.py:22
  165.1 3.6 %collective-permute-start.8 = (bf16[1,2,128,128]{3,2,1,0:T(8,128)(2,1)S(1)}, bf16[1,2,128,128]{3,2,1,0:T(8,128)(2,1)S(1)}, u32[]{:S(2)}, u32[]{:S(2)}) collective-permute-start(bf16[1,2,128,128]{3,2,1,0:T(8,128)(2,1)S(1)} %get-tuple-element.21), channel_id=1, source_target_pairs={{1,0},{2,1},{3,2},{5,4},{6,5},{7,6},{9,8},{10,9},{11,10},{13,12},{... | collective-permute-start | bytes 196616 | tf_op jit(solution)/shard_map/ppermute | solution.py:22
  169.3 2.2 %collective-permute-start.9 = (bf16[1,2,128,128]{3,2,1,0:T(8,128)(2,1)S(1)}, bf16[1,2,128,128]{3,2,1,0:T(8,128)(2,1)S(1)}, u32[]{:S(2)}, u32[]{:S(2)}) collective-permute-start(bf16[1,2,128,128]{3,2,1,0:T(8,128)(2,1)S(1)} %fusion.47), channel_id=1, source_target_pairs={{0,1},{1,2},{2,3},{4,5},{5,6},{6,7},{8,9},{9,10},{10,11},{12,13},{... | collective-permute-start | bytes 196616 | tf_op jit(solution)/shard_map/ppermute | solution.py:19
  171.8 3.6 %collective-permute-done.9 = bf16[1,2,128,128]{3,2,1,0:T(8,128)(2,1)S(1)} collective-permute-done((bf16[1,2,128,128]{3,2,1,0:T(8,128)(2,1)S(1)}, bf16[1,2,128,128]{3,2,1,0:T(8,128)(2,1)S(1)}, u32[]{:S(2)}, u32[]{:S(2)}) %collective-permute-start.9) | collective-permute-done | bytes 65568 | tf_op jit(solution)/shard_map/ppermute | solution.py:19
  175.7 2.9 %collective-permute-start.11 = (bf16[1,2,128,128]{3,2,1,0:T(8,128)(2,1)S(1)}, bf16[1,2,128,128]{3,2,1,0:T(8,128)(2,1)S(1)}, u32[]{:S(2)}, u32[]{:S(2)}) collective-permute-start(bf16[1,2,128,128]{3,2,1,0:T(8,128)(2,1)S(1)} %fusion.48), channel_id=1, source_target_pairs={{0,8},{8,16},{16,24},{1,9},{9,17},{17,25},{2,10},{10,18},{18,26},{... | collective-permute-start | bytes 196616 | tf_op jit(solution)/shard_map/ppermute | solution.py:19
  178.9 3.9 %collective-permute-done.11 = bf16[1,2,128,128]{3,2,1,0:T(8,128)(2,1)S(1)} collective-permute-done((bf16[1,2,128,128]{3,2,1,0:T(8,128)(2,1)S(1)}, bf16[1,2,128,128]{3,2,1,0:T(8,128)(2,1)S(1)}, u32[]{:S(2)}, u32[]{:S(2)}) %collective-permute-start.11) | collective-permute-done | bytes 65568 | tf_op jit(solution)/shard_map/ppermute | solution.py:19
  190.7 3.0 %collective-permute-start.13 = (bf16[1,2,128,128]{3,2,1,0:T(8,128)(2,1)S(1)}, bf16[1,2,128,128]{3,2,1,0:T(8,128)(2,1)S(1)}, u32[]{:S(2)}, u32[]{:S(2)}) collective-permute-start(bf16[1,2,128,128]{3,2,1,0:T(8,128)(2,1)S(1)} %fusion.49), channel_id=1, source_target_pairs={{0,4},{1,5},{2,6},{3,7},{8,12},{9,13},{10,14},{11,15},{16,20},{17,... | collective-permute-start | bytes 196616 | tf_op jit(solution)/shard_map/ppermute | solution.py:19
  193.7 3.9 %collective-permute-start.15 = (bf16[1,2,128,128]{3,2,1,0:T(8,128)(2,1)S(1)}, bf16[1,2,128,128]{3,2,1,0:T(8,128)(2,1)S(1)}, u32[]{:S(2)}, u32[]{:S(2)}) collective-permute-start(bf16[1,2,128,128]{3,2,1,0:T(8,128)(2,1)S(1)} %fusion.50), channel_id=1, source_target_pairs={{0,1},{1,2},{2,3},{4,5},{5,6},{6,7},{8,9},{9,10},{10,11},{12,13},{... | collective-permute-start | bytes 196616 | tf_op jit(solution)/shard_map/ppermute | solution.py:19
  197.9 3.9 %collective-permute-start.17 = (bf16[1,2,128,128]{3,2,1,0:T(8,128)(2,1)S(1)}, bf16[1,2,128,128]{3,2,1,0:T(8,128)(2,1)S(1)}, u32[]{:S(2)}, u32[]{:S(2)}) collective-permute-start(bf16[1,2,128,128]{3,2,1,0:T(8,128)(2,1)S(1)} %fusion.51), channel_id=1, source_target_pairs={{0,8},{8,16},{16,24},{1,9},{9,17},{17,25},{2,10},{10,18},{18,26},{... | collective-permute-start | bytes 196616 | tf_op jit(solution)/shard_map/ppermute | solution.py:19
  202.5 2.5 %collective-permute-done.17 = bf16[1,2,128,128]{3,2,1,0:T(8,128)(2,1)S(1)} collective-permute-done((bf16[1,2,128,128]{3,2,1,0:T(8,128)(2,1)S(1)}, bf16[1,2,128,128]{3,2,1,0:T(8,128)(2,1)S(1)}, u32[]{:S(2)}, u32[]{:S(2)}) %collective-permute-start.17) | collective-permute-done | bytes 65568 | tf_op jit(solution)/shard_map/ppermute | solution.py:19
  205.1 3.0 %fusion.61 = f32[1,1,1,2,1024,128]{5,4,3,2,1,0:T(8,128)} fusion(f32[1,1,1,2,1024,128]{5,4,3,2,1,0:T(8,128)S(1)} %broadcast_dynamic-update-slice_fusion.2, f32[1,1,1,1,1024,128]{5,4,3,2,1,0:T(8,128)S(1)} %fusion.25, f32[1,1,1,1,1024,128]{5,4,3,2,1,0:T(8,128)S(1)} %fusion.22, f32[1,1,1,2,1024,128]{5,4,3,2,1,0:T(8,128)S(1)} %broadcast_dynamic-update-slice_fusion.3, ...), kind=kLoop, calls=%fused_computation.80 | loop fusion | flops 5767168 | bytes 8388608 | tf_op jit(solution)/shard_map/add | solution.py:132
  (99 shorter events, 28.6 us)
Async XLA Ops:
  6.5 94.1 %reduce-scatter.2.cloned.1.call-start = ((), (), s32[]{:S(2)}) async-start(), calls=%async_computation.1 | async-start | bytes 5242880 | tf_op jit(solution)/shard_map/reduce_scatter | solution.py:58
  22.5 78.1 %copy-start.2 = (f32[1,256,1024]{2,1,0:T(8,128)S(1)}, f32[1,256,1024]{2,1,0:T(8,128)}, u32[]{:S(2)}) copy-start(f32[1,256,1024]{2,1,0:T(8,128)} %param.9) | copy-start | bytes 3145732
  22.5 80.3 %copy-start.1 = (f32[1,1,1,2,1024,128]{5,4,3,2,1,0:T(8,128)S(1)}, f32[1,1,1,2,1024,128]{5,4,3,2,1,0:T(8,128)}, u32[]{:S(2)}) copy-start(f32[1,1,1,2,1024,128]{5,4,3,2,1,0:T(8,128)} %param.13) | copy-start | bytes 3145732
  22.5 81.3 %copy-start.4 = (s32[1,1,1,3,2]{3,4,2,1,0:T(2,128)S(1)}, s32[1,1,1,3,2]{3,4,2,1,0:T(2,128)}, u32[]{:S(2)}) copy-start(s32[1,1,1,3,2]{3,4,2,1,0:T(2,128)} %param.11) | copy-start | bytes 76
  22.5 81.5 %copy-start.5 = (s32[1,1,1,3,2,128]{5,4,3,2,1,0:T(2,128)S(1)}, s32[1,1,1,3,2,128]{5,4,3,2,1,0:T(2,128)}, u32[]{:S(2)}) copy-start(s32[1,1,1,3,2,128]{5,4,3,2,1,0:T(2,128)} %param.12) | copy-start | bytes 9220
  22.6 128.0 %all-gather.2.cloned.1.call-start = ((), (), s32[]{:S(2)}) async-start(), calls=%async_computation.2 | async-start | bytes 4718592 | tf_op jit(solution)/shard_map/all_gather | solution.py:67
  105.1 16.7 %collective-permute-start.1 = (bf16[1,2,128,128]{3,2,1,0:T(8,128)(2,1)}, bf16[1,2,128,128]{3,2,1,0:T(8,128)(2,1)S(1)}, u32[]{:S(2)}, u32[]{:S(2)}) collective-permute-start(bf16[1,2,128,128]{3,2,1,0:T(8,128)(2,1)} %fusion.43), channel_id=1, source_target_pairs={{0,4},{1,5},{2,6},{3,7},{8,12},{9,13},{10,14},{11,15},{16,20},{17,... | collective-permute-start | bytes 196616 | tf_op jit(solution)/shard_map/ppermute | solution.py:19
  107.5 26.6 %collective-permute-start.4 = (bf16[1,2,128,128]{3,2,1,0:T(8,128)(2,1)}, bf16[1,2,128,128]{3,2,1,0:T(8,128)(2,1)S(1)}, u32[]{:S(2)}, u32[]{:S(2)}) collective-permute-start(bf16[1,2,128,128]{3,2,1,0:T(8,128)(2,1)} %get-tuple-element.29), channel_id=1, source_target_pairs={{8,0},{16,8},{24,16},{9,1},{17,9},{25,17},{10,2},{18,10},{26,18},{... | collective-permute-start | bytes 196616 | tf_op jit(solution)/shard_map/ppermute | solution.py:22
  110.8 16.3 %collective-permute-start.2 = (bf16[1,2,128,128]{3,2,1,0:T(8,128)(2,1)}, bf16[1,2,128,128]{3,2,1,0:T(8,128)(2,1)S(1)}, u32[]{:S(2)}, u32[]{:S(2)}) collective-permute-start(bf16[1,2,128,128]{3,2,1,0:T(8,128)(2,1)} %get-tuple-element.30), channel_id=1, source_target_pairs={{1,0},{2,1},{3,2},{5,4},{6,5},{7,6},{9,8},{10,9},{11,10},{13,12},{... | collective-permute-start | bytes 196616 | tf_op jit(solution)/shard_map/ppermute | solution.py:22
  113.0 7.1 %collective-permute-start = (bf16[1,2,128,128]{3,2,1,0:T(8,128)(2,1)S(1)}, bf16[1,2,128,128]{3,2,1,0:T(8,128)(2,1)S(1)}, u32[]{:S(2)}, u32[]{:S(2)}) collective-permute-start(bf16[1,2,128,128]{3,2,1,0:T(8,128)(2,1)S(1)} %get-tuple-element.31), channel_id=1, source_target_pairs={{4,0},{5,1},{6,2},{7,3},{12,8},{13,9},{14,10},{15,11},{20,16},{21,... | collective-permute-start | bytes 196616 | tf_op jit(solution)/shard_map/ppermute | solution.py:22
  122.2 8.4 %collective-permute-start.3 = (bf16[1,2,128,128]{3,2,1,0:T(8,128)(2,1)S(1)}, bf16[1,2,128,128]{3,2,1,0:T(8,128)(2,1)S(1)}, u32[]{:S(2)}, u32[]{:S(2)}) collective-permute-start(bf16[1,2,128,128]{3,2,1,0:T(8,128)(2,1)S(1)} %fusion.44), channel_id=1, source_target_pairs={{0,1},{1,2},{2,3},{4,5},{5,6},{6,7},{8,9},{9,10},{10,11},{12,13},{... | collective-permute-start | bytes 196616 | tf_op jit(solution)/shard_map/ppermute | solution.py:19
  130.9 7.1 %collective-permute-start.5 = (bf16[1,2,128,128]{3,2,1,0:T(8,128)(2,1)S(1)}, bf16[1,2,128,128]{3,2,1,0:T(8,128)(2,1)S(1)}, u32[]{:S(2)}, u32[]{:S(2)}) collective-permute-start(bf16[1,2,128,128]{3,2,1,0:T(8,128)(2,1)S(1)} %fusion.45), channel_id=1, source_target_pairs={{0,8},{8,16},{16,24},{1,9},{9,17},{17,25},{2,10},{10,18},{18,26},{... | collective-permute-start | bytes 196616 | tf_op jit(solution)/shard_map/ppermute | solution.py:19
  157.2 11.5 %collective-permute-start.6 = (bf16[1,2,128,128]{3,2,1,0:T(8,128)(2,1)S(1)}, bf16[1,2,128,128]{3,2,1,0:T(8,128)(2,1)S(1)}, u32[]{:S(2)}, u32[]{:S(2)}) collective-permute-start(bf16[1,2,128,128]{3,2,1,0:T(8,128)(2,1)S(1)} %get-tuple-element.22), channel_id=1, source_target_pairs={{4,0},{5,1},{6,2},{7,3},{12,8},{13,9},{14,10},{15,11},{20,16},{21,... | collective-permute-start | bytes 196616 | tf_op jit(solution)/shard_map/ppermute | solution.py:22
  158.8 10.1 %collective-permute-start.7 = (bf16[1,2,128,128]{3,2,1,0:T(8,128)(2,1)S(1)}, bf16[1,2,128,128]{3,2,1,0:T(8,128)(2,1)S(1)}, u32[]{:S(2)}, u32[]{:S(2)}) collective-permute-start(bf16[1,2,128,128]{3,2,1,0:T(8,128)(2,1)S(1)} %fusion.46), channel_id=1, source_target_pairs={{0,4},{1,5},{2,6},{3,7},{8,12},{9,13},{10,14},{11,15},{16,20},{17,... | collective-permute-start | bytes 196616 | tf_op jit(solution)/shard_map/ppermute | solution.py:19
  161.8 16.8 %collective-permute-start.10 = (bf16[1,2,128,128]{3,2,1,0:T(8,128)(2,1)S(1)}, bf16[1,2,128,128]{3,2,1,0:T(8,128)(2,1)S(1)}, u32[]{:S(2)}, u32[]{:S(2)}) collective-permute-start(bf16[1,2,128,128]{3,2,1,0:T(8,128)(2,1)S(1)} %get-tuple-element.20), channel_id=1, source_target_pairs={{8,0},{16,8},{24,16},{9,1},{17,9},{25,17},{10,2},{18,10},{26,18},{... | collective-permute-start | bytes 196616 | tf_op jit(solution)/shard_map/ppermute | solution.py:22
  165.1 6.4 %collective-permute-start.8 = (bf16[1,2,128,128]{3,2,1,0:T(8,128)(2,1)S(1)}, bf16[1,2,128,128]{3,2,1,0:T(8,128)(2,1)S(1)}, u32[]{:S(2)}, u32[]{:S(2)}) collective-permute-start(bf16[1,2,128,128]{3,2,1,0:T(8,128)(2,1)S(1)} %get-tuple-element.21), channel_id=1, source_target_pairs={{1,0},{2,1},{3,2},{5,4},{6,5},{7,6},{9,8},{10,9},{11,10},{13,12},{... | collective-permute-start | bytes 196616 | tf_op jit(solution)/shard_map/ppermute | solution.py:22
  169.3 6.2 %collective-permute-start.9 = (bf16[1,2,128,128]{3,2,1,0:T(8,128)(2,1)S(1)}, bf16[1,2,128,128]{3,2,1,0:T(8,128)(2,1)S(1)}, u32[]{:S(2)}, u32[]{:S(2)}) collective-permute-start(bf16[1,2,128,128]{3,2,1,0:T(8,128)(2,1)S(1)} %fusion.47), channel_id=1, source_target_pairs={{0,1},{1,2},{2,3},{4,5},{5,6},{6,7},{8,9},{9,10},{10,11},{12,13},{... | collective-permute-start | bytes 196616 | tf_op jit(solution)/shard_map/ppermute | solution.py:19
  175.7 7.1 %collective-permute-start.11 = (bf16[1,2,128,128]{3,2,1,0:T(8,128)(2,1)S(1)}, bf16[1,2,128,128]{3,2,1,0:T(8,128)(2,1)S(1)}, u32[]{:S(2)}, u32[]{:S(2)}) collective-permute-start(bf16[1,2,128,128]{3,2,1,0:T(8,128)(2,1)S(1)} %fusion.48), channel_id=1, source_target_pairs={{0,8},{8,16},{16,24},{1,9},{9,17},{17,25},{2,10},{10,18},{18,26},{... | collective-permute-start | bytes 196616 | tf_op jit(solution)/shard_map/ppermute | solution.py:19
  184.9 17.5 %collective-permute-start.16 = (bf16[1,2,128,128]{3,2,1,0:T(8,128)(2,1)S(1)}, bf16[1,2,128,128]{3,2,1,0:T(8,128)(2,1)S(1)}, u32[]{:S(2)}, u32[]{:S(2)}) collective-permute-start(bf16[1,2,128,128]{3,2,1,0:T(8,128)(2,1)S(1)} %get-tuple-element.15), channel_id=1, source_target_pairs={{8,0},{16,8},{24,16},{9,1},{17,9},{25,17},{10,2},{18,10},{26,18},{... | collective-permute-start | bytes 196616 | tf_op jit(solution)/shard_map/ppermute | solution.py:22
  186.8 15.3 %collective-permute-start.14 = (bf16[1,2,128,128]{3,2,1,0:T(8,128)(2,1)S(1)}, bf16[1,2,128,128]{3,2,1,0:T(8,128)(2,1)S(1)}, u32[]{:S(2)}, u32[]{:S(2)}) collective-permute-start(bf16[1,2,128,128]{3,2,1,0:T(8,128)(2,1)S(1)} %get-tuple-element.16), channel_id=1, source_target_pairs={{1,0},{2,1},{3,2},{5,4},{6,5},{7,6},{9,8},{10,9},{11,10},{13,12},{... | collective-permute-start | bytes 196616 | tf_op jit(solution)/shard_map/ppermute | solution.py:22
  188.7 9.2 %collective-permute-start.12 = (bf16[1,2,128,128]{3,2,1,0:T(8,128)(2,1)S(1)}, bf16[1,2,128,128]{3,2,1,0:T(8,128)(2,1)S(1)}, u32[]{:S(2)}, u32[]{:S(2)}) collective-permute-start(bf16[1,2,128,128]{3,2,1,0:T(8,128)(2,1)S(1)} %get-tuple-element.17), channel_id=1, source_target_pairs={{4,0},{5,1},{6,2},{7,3},{12,8},{13,9},{14,10},{15,11},{20,16},{21,... | collective-permute-start | bytes 196616 | tf_op jit(solution)/shard_map/ppermute | solution.py:22
  190.7 11.4 %collective-permute-start.13 = (bf16[1,2,128,128]{3,2,1,0:T(8,128)(2,1)S(1)}, bf16[1,2,128,128]{3,2,1,0:T(8,128)(2,1)S(1)}, u32[]{:S(2)}, u32[]{:S(2)}) collective-permute-start(bf16[1,2,128,128]{3,2,1,0:T(8,128)(2,1)S(1)} %fusion.49), channel_id=1, source_target_pairs={{0,4},{1,5},{2,6},{3,7},{8,12},{9,13},{10,14},{11,15},{16,20},{17,... | collective-permute-start | bytes 196616 | tf_op jit(solution)/shard_map/ppermute | solution.py:19
  193.7 8.6 %collective-permute-start.15 = (bf16[1,2,128,128]{3,2,1,0:T(8,128)(2,1)S(1)}, bf16[1,2,128,128]{3,2,1,0:T(8,128)(2,1)S(1)}, u32[]{:S(2)}, u32[]{:S(2)}) collective-permute-start(bf16[1,2,128,128]{3,2,1,0:T(8,128)(2,1)S(1)} %fusion.50), channel_id=1, source_target_pairs={{0,1},{1,2},{2,3},{4,5},{5,6},{6,7},{8,9},{9,10},{10,11},{12,13},{... | collective-permute-start | bytes 196616 | tf_op jit(solution)/shard_map/ppermute | solution.py:19
  197.9 7.1 %collective-permute-start.17 = (bf16[1,2,128,128]{3,2,1,0:T(8,128)(2,1)S(1)}, bf16[1,2,128,128]{3,2,1,0:T(8,128)(2,1)S(1)}, u32[]{:S(2)}, u32[]{:S(2)}) collective-permute-start(bf16[1,2,128,128]{3,2,1,0:T(8,128)(2,1)S(1)} %fusion.51), channel_id=1, source_target_pairs={{0,8},{8,16},{16,24},{1,9},{9,17},{17,25},{2,10},{10,18},{18,26},{... | collective-permute-start | bytes 196616 | tf_op jit(solution)/shard_map/ppermute | solution.py:19
  (2 other events, 3.5 us)
Sparse Core Ops, SparseCore 0:
  22.7 77.8 reduce-scatter.1
  103.0 47.5 all-gather.1
where the time goes:
time: 216 us; the launch traced here: 215 us
  waiting for transfers between devices  105 us (49%)
  starting transfers between devices  47 us (22%)
  matrix products  29.5 us (14%)
  between operations  18.1 us (8%)
  other arithmetic  9.75 us (5%)
  local copies, waits for them, and re-layouts  5.78 us (3%)
    reduce_scatter x1, waiting for transfers between devices, per_device(): lax.psum_scatter(lax.dot_general(scaled, own_modes, (((1,), (1,)), ((), (...  78 us
    ppermute x9, starting transfers between devices, with_halo(): lax.ppermute(lax.slice_in_dim(block, block.shape[dim] - width, None, axis...  26.9 us
    ppermute x9, starting transfers between devices, with_halo(): lax.ppermute(lax.slice_in_dim(block, 0, width, axis=dim), axis, backward)  20.1 us
    dot_general x1, matrix products, per_device(): lax.dot_general(scaled, own_modes, (((1,), (1,)), ((), ())), preferred_el...  16 us
    ppermute x9, waiting for transfers between devices, with_halo(): lax.ppermute(lax.slice_in_dim(block, block.shape[dim] - width, None, axis...  15.5 us
    all_gather x1, waiting for transfers between devices, per_device(): stacked_rows = lax.all_gather(blocks, ('inst', 'face'), axis=0, tiled=True)  11.2 us
    dot_general x6, matrix products, operator_apply(): jnp.dot(matrices[number], lowered[number], preferred_element_type=jnp.flo...  7.56 us
  transfers between devices with their start and end apart: 20, of which 7 were waited for; matrix products, arithmetic and copies ran while one was open for 7% of the time, Pallas kernels for 0%

commit v1 on v0

v1 whole, which is shorter than its diff:
```python
import jax
import jax.numpy as jnp
from jax import lax
from jax.experimental import pallas as pl
from jax.experimental.pallas import tpu as pltpu
from jax.sharding import PartitionSpec as P

SIDES = 8
lower_bound = 2.0
upper_bound = 12.0
theta = (upper_bound + lower_bound) / 2.0
delta = (upper_bound - lower_bound) / 2.0
sigma = theta / delta
w0 = 1.0 / sigma
w1 = 1.0 / (2.0 * sigma - w0)
w2 = 1.0 / (2.0 * sigma - w1)
w3 = 1.0 / (2.0 * sigma - w2)
keep = (w1 * w0, w2 * w1, w3 * w2)
gain = (2.0 * w1 / delta, 2.0 * w2 / delta, 2.0 * w3 / delta)

AXES = ("inst", "face", "types")
F32 = jnp.float32
BF16 = jnp.bfloat16
VMEM = pl.BlockSpec(memory_space=pltpu.VMEM)
SMEM = pl.BlockSpec(memory_space=pltpu.SMEM)


def dot(a, b):
    return lax.dot_general(a, b, (((1,), (0,)), ((), ())), preferred_element_type=F32)


def dot_nt(a, b):
    return lax.dot_general(a, b, (((1,), (1,)), ((), ())), preferred_element_type=F32)


def shape_of(dims, dtype):
    return jax.ShapeDtypeStruct(dims, dtype)


def call(body, out_shape, operands, specs, flops, name):
    moved = sum(x.size * x.dtype.itemsize for x in operands)
    return pl.pallas_call(
        body,
        out_shape=out_shape,
        in_specs=specs,
        out_specs=jax.tree.map(lambda _: VMEM, out_shape),
        cost_estimate=pl.CostEstimate(flops=flops, bytes_accessed=moved, transcendentals=0),
        name=name,
    )(*operands)


def owned_boundary(bd_ref, row, count, face):
    held = bd_ref.shape[0]
    step = min(held, count)
    parts = []
    for start in range(row, row + count, step):
        local = bd_ref[start % held : start % held + step, :]
        parts.append(jnp.where(face == start // held, local, 0.0))
    return parts[0] if len(parts) == 1 else jnp.concatenate(parts, axis=0)


def modal_blocks(modes, stiffness, boundary, pairs, packed, name):
    nb, depth = modes.shape
    block = 2 * nb // SIDES
    half = block // 2
    count = nb // block
    tile = min(1024, depth)
    steps = depth // tile
    rows = sorted({i for pair in pairs for i in pair})
    lefts = sorted({i for i, _ in pairs})
    if packed:
        height = half * ((count + 1) // 2)
        extra = 16 * ((2 * count + 15) // 16)
        out_rows = 2 * height + extra
    else:
        out_rows = block * len(pairs)

    def body(*refs):
        k_ref = refs[0]
        c_refs = dict(zip(rows, refs[1 : 1 + len(rows)]))
        b_refs = refs[1 + len(rows) : 1 + len(rows) + len(pairs)]
        out_ref, acc_ref = refs[-2:]
        step = pl.program_id(0)
        inverse = 1.0 / k_ref[...]
        left = {i: (c_refs[i][...].astype(F32) * inverse).astype(BF16) for i in lefts}
        for n, (i, j) in enumerate(pairs):
            part = dot_nt(left[i], c_refs[j][...])

            @pl.when(step == 0)
            def _():
                acc_ref[n] = part

            @pl.when(step > 0)
            def _():
                acc_ref[n] += part

        @pl.when(step == steps - 1)
        def _():
            face = lax.axis_index("face")
            if not packed:
                for n, (i, j) in enumerate(pairs):
                    held = owned_boundary(b_refs[n], i * block, block, face)
                    out_ref[n * block : (n + 1) * block, :] = (held - acc_ref[n]).astype(BF16)
                return
            r = lax.broadcasted_iota(jnp.int32, (half, half), 0)
            c = lax.broadcasted_iota(jnp.int32, (half, half), 1)
            rr = lax.broadcasted_iota(jnp.int32, (block, block), 0)
            cc = lax.broadcasted_iota(jnp.int32, (block, block), 1)
            highs, rests = [], []
            for n, (i, _) in enumerate(pairs):
                held = owned_boundary(b_refs[n], i * block, block, face)
                acc = acc_ref[n]
                diff = held - acc
                own = jnp.sum(jnp.where(rr == cc, held, 0.0), axis=0, keepdims=True)
                modal = jnp.sum(jnp.where(rr == cc, acc, 0.0), axis=0, keepdims=True)
                high = own.astype(BF16).astype(F32)
                highs.append(high)
                rests.append((own - high) - modal)
                a = diff[:half, :half]
                b = diff[half:, half:]
                both = jnp.where(r < c, a, jnp.where(r > c, b, 0.0))
                top, side = half * (n // 2), half * (n % 2)
                out_ref[top : top + half, side : side + half] = both.astype(BF16)
                out_ref[height + top : height + top + half, side : side + half] = diff[
                    :half, half:
                ].astype(BF16)
            fill = [jnp.zeros((extra - 2 * count, block), F32)] if extra > 2 * count else []
            out_ref[2 * height :, :] = jnp.concatenate(highs + rests + fill, axis=0).astype(BF16)

    def row_spec(i):
        return pl.BlockSpec((block, tile), lambda k, i=i: (i, k))

    def boundary_spec(j):
        return pl.BlockSpec((boundary.shape[0], block), lambda k, j=j: (0, j))

    return pl.pallas_call(
        body,
        grid=(steps,),
        out_shape=shape_of((out_rows, block), BF16),
        in_specs=[pl.BlockSpec((1, tile), lambda k: (0, k))]
        + [row_spec(i) for i in rows]
        + [boundary_spec(j) for _, j in pairs],
        out_specs=pl.BlockSpec((out_rows, block), lambda k: (0, 0)),
        scratch_shapes=[pltpu.VMEM((len(pairs), block, block), F32)],
        cost_estimate=pl.CostEstimate(
            flops=2 * len(pairs) * block * block * depth,
            bytes_accessed=2 * len(rows) * block * depth,
            transcendentals=0,
        ),
        name=name,
    )(stiffness, *([modes] * len(rows)), *([boundary] * len(pairs)))


def unpack_diagonal(packed_list, count):
    block = packed_list[0].shape[1]
    half = block // 2
    height = half * ((count + 1) // 2)

    def body(*refs):
        total = len(refs) // 2
        r = lax.broadcasted_iota(jnp.int32, (half, half), 0)
        c = lax.broadcasted_iota(jnp.int32, (half, half), 1)
        for p_ref, d_ref in zip(refs[:total], refs[total:]):
            lines = p_ref[2 * height :, :].astype(F32)
            for i in range(count):
                line = lines[i : i + 1, :] + lines[count + i : count + i + 1, :]
                top, side = half * (i // 2), half * (i % 2)
                both = p_ref[top : top + half, side : side + half].astype(F32)
                off = p_ref[height + top : height + top + half, side : side + half]
                upper = jnp.where(r < c, both, 0.0)
                lower = jnp.where(r > c, both, 0.0)
                a = upper + upper.T + jnp.where(r == c, line[:, :half], 0.0)
                b = lower + lower.T + jnp.where(r == c, line[:, half:], 0.0)
                d_ref[i, :half, :half] = a.astype(BF16)
                d_ref[i, half:, half:] = b.astype(BF16)
                d_ref[i, :half, half:] = off
                d_ref[i, half:, :half] = off.astype(F32).T.astype(BF16)

    return call(
        body,
        [shape_of((count, block, block), BF16) for _ in packed_list],
        packed_list,
        [VMEM] * len(packed_list),
        10_000_000,
        "unpack_diagonal",
    )


def parity_and_masks(axis):
    index = lax.axis_index(axis)
    return index % 2 == 0, index < lax.axis_size(axis) - 1, index > 0


def side_pair(values, e, port):
    upper = [v[:, 2 * e * port : (2 * e + 1) * port] for v in values]
    lower = [v[:, (2 * e + 1) * port : (2 * e + 2) * port] for v in values]
    return jnp.concatenate(upper, axis=1), jnp.concatenate(lower, axis=1)


def write_sends(values, port, match_ref, send_refs):
    at = 0
    for e, axis in enumerate(AXES):
        even, _, _ = parity_and_masks(axis)
        upper, lower = side_pair(values, e, port)
        outgoing = dot_nt(upper.astype(BF16), match_ref[e])
        lower = lower.astype(BF16).astype(F32)
        send_refs[at][...] = jnp.where(even, outgoing, lower).astype(BF16)
        at += 1
        if lax.axis_size(axis) > 2:
            send_refs[at][...] = jnp.where(even, lower, outgoing).astype(BF16)
            at += 1


def arrivals(recv_refs):
    at = 0
    out = []
    for axis in AXES:
        even, has_next, has_prev = parity_and_masks(axis)
        first = recv_refs[at][...].astype(F32)
        at += 1
        if lax.axis_size(axis) > 2:
            second = recv_refs[at][...].astype(F32)
            at += 1
            after, before = jnp.where(even, first, second), jnp.where(even, second, first)
        else:
            after, before = first, first
        after = jnp.where(has_next, after, 0.0)
        before = jnp.where(has_prev, before, 0.0)
        out.append((after, before, has_next, has_prev))
    return out


def exchange(sends):
    at = 0
    out = []
    for axis in AXES:
        size = lax.axis_size(axis)
        for first in (0, 1) if size > 2 else (0,):
            swaps = []
            for p in range(first, size - 1, 2):
                swaps += [(p, p + 1), (p + 1, p)]
            out.append(lax.ppermute(sends[at], axis, swaps))
            at += 1
    return out


def send_shapes(load_count, width):
    total = sum(2 if lax.axis_size(axis) > 2 else 1 for axis in AXES)
    return [shape_of((load_count, width), BF16) for _ in range(total)]


def own_terms(values, port):
    sides = []
    for axis in AXES:
        _, has_next, has_prev = parity_and_masks(axis)
        sides += [has_next, has_prev]
    out = []
    for v in values:
        parts = [
            jnp.where(sides[k], v[:, k * port : (k + 1) * port], 0.0) for k in range(len(sides))
        ]
        parts.append(jnp.zeros((v.shape[0], v.shape[1] - len(sides) * port), F32))
        out.append(jnp.concatenate(parts, axis=1))
    return out


def arrival_terms(recv_refs, match_ref, slot_total, port, nb):
    parts = [[] for _ in range(slot_total)]
    for e, (after, before, _, _) in enumerate(arrivals(recv_refs)):
        partner = dot(after.astype(BF16), match_ref[e])
        for s in range(slot_total):
            parts[s] += [partner[:, s * port : (s + 1) * port], before[:, s * port : (s + 1) * port]]
    out = []
    for s in range(slot_total):
        rest = nb - 2 * len(AXES) * port
        parts[s].append(jnp.zeros((parts[s][0].shape[0], rest), F32))
        out.append(jnp.concatenate(parts[s], axis=1))
    return out


def per_device(
    coupling_modes, mode_stiffness, boundary_stiffness, slot_type, partner_slot, port_map, loads
):
    modes = coupling_modes[0]
    nb = modes.shape[0]
    boundary = boundary_stiffness[0]
    rhs = loads[0, 0, 0]
    slot_total, _, load_count = rhs.shape
    kinds = slot_type[0, 0, 0]
    partners = partner_slot[0, 0, 0]
    ports = port_map[0, 0, 0]
    port = nb // SIDES
    block = 2 * port
    count = nb // block
    width = slot_total * port
    insts = lax.axis_size("inst")
    faces = lax.axis_size("face")
    vec = (slot_total, load_count, nb)

    def prepare(loads_ref, partner_ref, ports_ref, b_ref, match_ref, back_ref, *send_refs):
        values = []
        for s in range(slot_total):
            b = loads_ref[s].T
            b_ref[s] = b
            values.append(b / theta)
        row = lax.broadcasted_iota(jnp.int32, (width, width), 0)
        for e in range(len(AXES)):
            target = jnp.concatenate(
                [partner_ref[e, s] * port + ports_ref[e, s : s + 1, :] for s in range(slot_total)],
                axis=1,
            )
            table = (row == target).astype(F32)
            match_ref[e] = table.astype(BF16)
            back_ref[e] = table.T.astype(BF16)
        write_sends(values, port, match_ref, send_refs)

    tables = shape_of((len(AXES), width, width), BF16)
    bt, match, back, *sends = call(
        prepare,
        [shape_of(vec, F32), tables, tables] + send_shapes(load_count, width),
        (rhs, partners, ports),
        [VMEM, SMEM, VMEM],
        200_000_000,
        "prepare",
    )

    stiffness = mode_stiffness[0][None, :]
    offs = [(i, j) for j in range(count) for i in range(j)]
    diag = [(i, i) for i in range(count)]
    middle = offs[1:-1]
    plan = [(offs[:1], False), (diag, True)]
    plan += [(middle[k : k + 2], False) for k in range(0, len(middle), 2)]
    plan += [(offs[-1:], False)]
    partial_sums = [
        modal_blocks(modes, stiffness, boundary, pairs, packed, f"modal_{n}")
        for n, (pairs, packed) in enumerate(plan)
    ]

    def add(a, b):
        return (a.astype(F32) + b.astype(F32)).astype(BF16)

    def over_faces(part):
        if faces != 4:
            return lax.psum(part.astype(F32), "face").astype(BF16)
        z = lax.axis_index("face")
        inner = (z == 1) | (z == 2)
        left = add(part, lax.ppermute(part, "face", [(0, 1), (3, 2)]))
        total = add(left, lax.ppermute(left, "face", [(1, 2), (2, 1)]))
        spread = lax.ppermute(total, "face", [(1, 0), (2, 3)])
        return jnp.where(inner, total, spread)

    summed = [over_faces(part) for part in partial_sums]

    if insts == 2:
        candidates = [(own, lax.ppermute(own, "inst", [(0, 1), (1, 0)])) for own in summed]
    else:
        candidates = []
        for own in summed:
            stack = lax.all_gather(own, "inst", axis=0)
            candidates.append(
                tuple(
                    lax.dynamic_index_in_dim(stack, kinds[s], 0, keepdims=False)
                    for s in range(slot_total)
                )
            )
    options = len(candidates[0])
    candidates[1] = tuple(unpack_diagonal(list(candidates[1]), count))

    def each_option(kind_ref, use):
        me = lax.axis_index("inst")
        for s in range(slot_total):
            for option in range(options):
                if insts == 2:
                    hit = (kind_ref[s] == me) if option == 0 else (kind_ref[s] != me)
                    pl.when(hit)(lambda s=s, option=option: use(s, option))
                elif option == s:
                    use(s, option)

    def products(x, chunk_ids, chunk_refs):
        acc = [None] * count

        def gather(j, v):
            acc[j] = v if acc[j] is None else acc[j] + v

        cols = [x[:, i * block : (i + 1) * block] for i in range(count)]
        for n, ref in zip(chunk_ids, chunk_refs):
            pairs, packed = plan[n]
            for at, (i, j) in enumerate(pairs):
                if packed:
                    gather(i, dot(cols[i], ref[i]))
                else:
                    matrix = ref[at * block : (at + 1) * block, :]
                    gather(j, dot(cols[i], matrix))
                    gather(i, dot_nt(cols[j], matrix))
        return acc

    everything = list(range(len(plan)))
    flops_all = 2 * slot_total * load_count * nb * nb

    def matrices(ids):
        return [candidates[n][o] for o in range(options) for n in ids]

    def option_refs(refs, ids, option):
        return refs[option * len(ids) : (option + 1) * len(ids)]

    received = exchange(sends)

    def couple_first(b_ref, match_ref, *refs):
        out_ref = refs[-1]
        values = [b_ref[s] / theta for s in range(slot_total)]
        mine = own_terms(values, port)
        theirs = arrival_terms(refs[:-1], match_ref, slot_total, port, nb)
        for s in range(slot_total):
            out_ref[s] = b_ref[s] - mine[s] + theirs[s]

    r1_base = call(
        couple_first,
        shape_of(vec, F32),
        (bt, match, *received),
        [VMEM] * (2 + len(received)),
        50_000_000,
        "couple_first",
    )

    early, late = everything[:-1], everything[-1:]

    def first_product(b_ref, r_ref, kind_ref, *refs):
        out_ref = refs[-1]

        def use(s, option):
            x = (b_ref[s] / theta).astype(BF16)
            acc = products(x, early, option_refs(refs, early, option))
            for j in range(count):
                cols = slice(j * block, (j + 1) * block)
                out_ref[s, :, cols] = r_ref[s, :, cols] - acc[j]

        each_option(kind_ref, use)

    mats = matrices(early)
    r1_part = call(
        first_product,
        shape_of(vec, F32),
        (bt, r1_base, kinds, *mats),
        [VMEM, VMEM, SMEM] + [VMEM] * len(mats),
        flops_all,
        "first_product",
    )

    def first_finish(b_ref, r_ref, match_ref, kind_ref, *refs):
        refs, (r_out, d_out), send_refs = (
            refs[: options * len(late)],
            refs[options * len(late) : options * len(late) + 2],
            refs[options * len(late) + 2 :],
        )

        def use(s, option):
            x = (b_ref[s] / theta).astype(BF16)
            acc = products(x, late, option_refs(refs, late, option))
            for j in range(count):
                cols = slice(j * block, (j + 1) * block)
                r = r_ref[s, :, cols]
                if acc[j] is not None:
                    r = r - acc[j]
                r_out[s, :, cols] = r
                d_out[s, :, cols] = keep[0] * (b_ref[s, :, cols] / theta) + gain[0] * r

        each_option(kind_ref, use)
        write_sends([d_out[s] for s in range(slot_total)], port, match_ref, send_refs)

    mats = matrices(late)
    r1, d1, *sends = call(
        first_finish,
        [shape_of(vec, F32), shape_of(vec, F32)] + send_shapes(load_count, width),
        (bt, r1_part, match, kinds, *mats),
        [VMEM, VMEM, VMEM, SMEM] + [VMEM] * len(mats),
        flops_all // 4,
        "first_finish",
    )

    received = exchange(sends)
    mats = matrices(everything)

    def second_product(d_ref, r_ref, kind_ref, *refs):
        out_ref = refs[-1]

        def use(s, option):
            d = d_ref[s]
            acc = products(d.astype(BF16), everything, option_refs(refs, everything, option))
            base = r_ref[s] - own_terms([d], port)[0]
            for j in range(count):
                cols = slice(j * block, (j + 1) * block)
                out_ref[s, :, cols] = base[:, cols] - acc[j]

        each_option(kind_ref, use)

    r2_base = call(
        second_product,
        shape_of(vec, F32),
        (d1, r1, kinds, *mats),
        [VMEM, VMEM, SMEM] + [VMEM] * len(mats),
        flops_all,
        "second_product",
    )

    def second_finish(d_ref, r_ref, match_ref, *refs):
        total = len(received)
        recv_refs, r_out, d_out, send_refs = (
            refs[:total],
            refs[total],
            refs[total + 1],
            refs[total + 2 :],
        )
        theirs = arrival_terms(recv_refs, match_ref, slot_total, port, nb)
        values = []
        for s in range(slot_total):
            r = r_ref[s] + theirs[s]
            d = keep[1] * d_ref[s] + gain[1] * r
            r_out[s] = r
            d_out[s] = d
            values.append(d)
        write_sends(values, port, match_ref, send_refs)

    r2, d2, *sends = call(
        second_finish,
        [shape_of(vec, F32), shape_of(vec, F32)] + send_shapes(load_count, width),
        (d1, r2_base, match, *received),
        [VMEM] * (3 + len(received)),
        100_000_000,
        "second_finish",
    )

    received = exchange(sends)

    def third_product(b_ref, d1_ref, d_ref, r_ref, kind_ref, *refs):
        out_ref = refs[-1]

        def use(s, option):
            d = d_ref[s]
            acc = products(d.astype(BF16), everything, option_refs(refs, everything, option))
            base = r_ref[s] - own_terms([d], port)[0]
            sums = (b_ref[s] / theta + d1_ref[s]) + d
            for j in range(count):
                cols = slice(j * block, (j + 1) * block)
                last = keep[2] * d[:, cols] + gain[2] * (base[:, cols] - acc[j])
                out_ref[s, cols, :] = (sums[:, cols] + last).T

        each_option(kind_ref, use)

    x_base = call(
        third_product,
        shape_of(rhs.shape, F32),
        (bt, d1, d2, r2, kinds, *mats),
        [VMEM] * 4 + [SMEM] + [VMEM] * len(mats),
        flops_all,
        "third_product",
    )

    def third_finish(x_ref, back_ref, *refs):
        out_ref = refs[-1]
        row = lax.broadcasted_iota(jnp.int32, (width, width), 0)
        col = lax.broadcasted_iota(jnp.int32, (width, width), 1)
        unit = (row == col).astype(F32).astype(BF16)
        for e, (after, before, _, _) in enumerate(arrivals(refs[:-1])):
            partner = dot_nt(back_ref[e], after.astype(BF16))
            behind = dot_nt(unit, before.astype(BF16))
            for s in range(slot_total):
                for side, term in ((2 * e, partner), (2 * e + 1, behind)):
                    rows = slice(side * port, (side + 1) * port)
                    out_ref[s, rows, :] = (
                        x_ref[s, rows, :] + gain[2] * term[s * port : (s + 1) * port]
                    )
        for s in range(slot_total):
            rows = slice(2 * len(AXES) * port, nb)
            out_ref[s, rows, :] = x_ref[s, rows, :]

    displacement = call(
        third_finish,
        shape_of(rhs.shape, F32),
        (x_base, back, *received),
        [VMEM] * (2 + len(received)),
        100_000_000,
        "third_finish",
    )
    return displacement[None, None, None]


def solution(mesh):
    placed = (
        P(("types", "inst"), None, "face"),
        P(("types", "inst"), "face"),
        P(("types", "inst"), "face", None),
        P("types", "inst", "face", None),
        P("types", "inst", "face", None, None),
        P("types", "inst", "face", None, None, None),
        P("types", "inst", "face", None, None, None),
    )
    return jax.shard_map(
        per_device,
        mesh=mesh,
        in_specs=placed,
        out_specs=P("types", "inst", "face", None, None, None),
        check_vma=False,
    )
```

time: 216 us -> 161 us (0.75)
  waiting for transfers between devices: 105 us -> 25.2 us
  Pallas kernels: 0 us -> 67.8 us
  matrix products: 29.5 us -> 0 us
  between operations: 18.1 us -> 0.73 us
  starting transfers between devices: 47 us -> 59 us
  other arithmetic: 9.75 us -> 1.66 us
    reduce_scatter x1 -> x0, waiting for transfers between devices: 78 us -> none  [per_device(): lax.psum_scatter(lax.dot_general(scaled, own_modes, (((1,), (1,)), ((), (...]
    pallas_call x0 -> x14, Pallas kernels: none -> 67.8 us  [the longest x5 35.5 us: modal_blocks(): pl.pallas_call(body, grid=(steps,), out_shape=shape_of((out_rows, block),...]
    dot_general x25 -> x0, matrix products: 29.5 us -> none  [the longest x1 16 us: per_device(): lax.dot_general(scaled, own_modes, (((1,), (1,)), ((), ())), preferred_el...]
    ppermute x18 -> x35, starting transfers between devices: 47 us -> 59 us  [the longest x15 24 us: exchange(): out.append(lax.ppermute(sends[at], axis, swaps))]
    all_gather x1 -> x0, waiting for transfers between devices: 11.2 us -> none  [per_device(): stacked_rows = lax.all_gather(blocks, ('inst', 'face'), axis=0, tiled=True)]
    ppermute x18 -> x35, waiting for transfers between devices: 15.6 us -> 25.2 us  [the longest x5 16.6 us: over_faces(): total = add(left, lax.ppermute(left, 'face', [(1, 2), (2, 1)]))]
    add x2 -> x0, other arithmetic: 3.06 us -> none  [the longest x1 2.98 us: per_device(): displacement = displacement + direction]
    convert_element_type x4 -> x10, other arithmetic: 3.89 us -> 1.52 us  [add(): return (a.astype(F32) + b.astype(F32)).astype(BF16)]
  transfers between devices with their start and end apart: 20 -> 35, of which waited for: 7 -> 9; matrix products, arithmetic and copies ran while one was open for 7% -> 1% of each run, Pallas kernels for 0% -> 33%
where the time goes in v1:
time: 161 us; the launch traced here: 160 us
  Pallas kernels  67.8 us (42%)
  starting transfers between devices  59 us (37%)
  waiting for transfers between devices  25.2 us (16%)
  local copies, waits for them, and re-layouts  5.39 us (3%)
  other arithmetic  1.66 us (1%)
    pallas_call x5, Pallas kernels, modal_blocks(): pl.pallas_call(body, grid=(steps,), out_shape=shape_of((out_rows, block),...  35.5 us
    pallas_call x9, Pallas kernels, call(): pl.pallas_call(body, out_shape=out_shape, in_specs=specs, out_specs=jax.t...  32.2 us
    ppermute x15, starting transfers between devices, exchange(): out.append(lax.ppermute(sends[at], axis, swaps))  24 us
    ppermute x5, waiting for transfers between devices, over_faces(): total = add(left, lax.ppermute(left, 'face', [(1, 2), (2, 1)]))  16.6 us
    ppermute x5, starting transfers between devices, over_faces(): total = add(left, lax.ppermute(left, 'face', [(1, 2), (2, 1)]))  14.7 us
    ppermute x5, starting transfers between devices, over_faces(): spread = lax.ppermute(total, 'face', [(1, 0), (2, 3)])  12.7 us
    ppermute x5, starting transfers between devices, over_faces(): left = add(part, lax.ppermute(part, 'face', [(0, 1), (3, 2)]))  6.54 us
    ppermute x5, waiting for transfers between devices, over_faces(): spread = lax.ppermute(total, 'face', [(1, 0), (2, 3)])  5.89 us
  transfers between devices with their start and end apart: 35, of which 9 were waited for; matrix products, arithmetic and copies ran while one was open for 1% of the time, Pallas kernels for 33%

profile of v1, /device:TPU:12, one launch (start us, length us, event | category | flops | bytes accessed | tf_op | source)
XLA Modules:
  0.0 159.6 jit_solution(438510168602828174)
XLA Ops:
  0.0 4.6 %modal_0.1 = bf16[256,256]{1,0:T(8,128)(2,1)} custom-call(f32[1,4096]{1,0:T(1,128)} %refs_0_.9, bf16[1024,4096]{1,0:T(8,128)(2,1)} %bitcast.7, bf16[1024,4096]{1,0:T(8,128)(2,1)} %bitcast.8, f32[256,1024]{1,0:T(8,128)} %bitcast.21), custom_call_target="tpu_custom_call" | custom-call | flops 536870912 | bytes 4194304 | tf_op jit(solution)/shard_map/modal_0/pallas_call | solution.py:136
  5.9 4.6 %modal_4.1 = bf16[256,256]{1,0:T(8,128)(2,1)} custom-call(f32[1,4096]{1,0:T(1,128)} %refs_0_.9, bf16[1024,4096]{1,0:T(8,128)(2,1)} %bitcast.9, bf16[1024,4096]{1,0:T(8,128)(2,1)} %bitcast.10, f32[256,1024]{1,0:T(8,128)} %bitcast.22), custom_call_target="tpu_custom_call" | custom-call | flops 536870912 | bytes 4194304 | tf_op jit(solution)/shard_map/modal_4/pallas_call | solution.py:136
  11.8 7.1 %modal_2.1 = bf16[512,256]{1,0:T(8,128)(2,1)} custom-call(f32[1,4096]{1,0:T(1,128)} %refs_0_.9, bf16[1024,4096]{1,0:T(8,128)(2,1)} %bitcast.11, bf16[1024,4096]{1,0:T(8,128)(2,1)} %bitcast.12, bf16[1024,4096]{1,0:T(8,128)(2,1)} %bitcast.13, f32[256,1024]{1,0:T(8,128)} %bitcast.23, f32[256,1024]{1,0:T(8,128)} %bitcast.24), custom_call_target="tpu_custom_call" | custom-call | flops 1073741824 | bytes 6291456 | tf_op jit(solution)/shard_map/modal_2/pallas_call | solution.py:136
  20.2 7.1 %modal_3.1 = bf16[512,256]{1,0:T(8,128)(2,1)} custom-call(f32[1,4096]{1,0:T(1,128)} %refs_0_.9, bf16[1024,4096]{1,0:T(8,128)(2,1)} %bitcast.14, bf16[1024,4096]{1,0:T(8,128)(2,1)} %bitcast.15, bf16[1024,4096]{1,0:T(8,128)(2,1)} %bitcast.16, f32[256,1024]{1,0:T(8,128)} %bitcast.25, f32[256,1024]{1,0:T(8,128)} %bitcast.26), custom_call_target="tpu_custom_call" | custom-call | flops 1073741824 | bytes 6291456 | tf_op jit(solution)/shard_map/modal_3/pallas_call | solution.py:136
  28.8 12.1 %modal_1.1 = bf16[528,256]{1,0:T(8,128)(2,1)} custom-call(f32[1,4096]{1,0:T(1,128)} %refs_0_.9, bf16[1024,4096]{1,0:T(8,128)(2,1)} %bitcast.17, bf16[1024,4096]{1,0:T(8,128)(2,1)} %bitcast.18, bf16[1024,4096]{1,0:T(8,128)(2,1)} %bitcast.19, bf16[1024,4096]{1,0:T(8,128)(2,1)} %bitcast.20, f32[256,1024]{1,0:T(8,128)} %bitcast.27, f32[256,1024]{1,0:T(8,128)} %bitcast.28, ...), custom_call_target="tpu_custom_call" | custom-call | flops 2147483648 | bytes 8388608 | tf_op jit(solution)/shard_map/modal_1/pallas_call | solution.py:136
  48.7 3.5 %collective-permute-start.6 = (bf16[256,256]{1,0:T(8,128)(2,1)S(1)}, bf16[256,256]{1,0:T(8,128)(2,1)S(1)}, u32[]{:S(2)}, u32[]{:S(2)}) collective-permute-start(bf16[256,256]{1,0:T(8,128)(2,1)S(1)} %add_convert_fusion.9), channel_id=1, source_target_pairs={{1,2},{2,1},{5,6},{6,5},{9,10},{10,9},{13,14},{14,13},{17,18},{18,... | collective-permute-start | bytes 393224 | tf_op jit(solution)/shard_map/ppermute | solution.py:348
  52.3 3.9 %collective-permute-done.6 = bf16[256,256]{1,0:T(8,128)(2,1)S(1)} collective-permute-done((bf16[256,256]{1,0:T(8,128)(2,1)S(1)}, bf16[256,256]{1,0:T(8,128)(2,1)S(1)}, u32[]{:S(2)}, u32[]{:S(2)}) %collective-permute-start.6) | collective-permute-done | bytes 131104 | tf_op jit(solution)/shard_map/ppermute | solution.py:348
  56.2 3.5 %collective-permute-start.22 = (bf16[256,256]{1,0:T(8,128)(2,1)S(1)}, bf16[256,256]{1,0:T(8,128)(2,1)S(1)}, u32[]{:S(2)}, u32[]{:S(2)}) collective-permute-start(bf16[256,256]{1,0:T(8,128)(2,1)S(1)} %add_convert_fusion.7), channel_id=1, source_target_pairs={{1,2},{2,1},{5,6},{6,5},{9,10},{10,9},{13,14},{14,13},{17,18},{18,... | collective-permute-start | bytes 393224 | tf_op jit(solution)/shard_map/ppermute | solution.py:348
  59.7 3.3 %collective-permute-done.22 = bf16[256,256]{1,0:T(8,128)(2,1)S(1)} collective-permute-done((bf16[256,256]{1,0:T(8,128)(2,1)S(1)}, bf16[256,256]{1,0:T(8,128)(2,1)S(1)}, u32[]{:S(2)}, u32[]{:S(2)}) %collective-permute-start.22) | collective-permute-done | bytes 131104 | tf_op jit(solution)/shard_map/ppermute | solution.py:348
  63.1 3.5 %collective-permute-start.2 = (bf16[128,256]{1,0:T(8,128)(2,1)}, bf16[128,256]{1,0:T(8,128)(2,1)S(1)}, u32[]{:S(2)}, u32[]{:S(2)}) collective-permute-start(bf16[128,256]{1,0:T(8,128)(2,1)} %get-tuple-element.33), channel_id=1, source_target_pairs={{1,2},{2,1},{5,6},{6,5},{9,10},{10,9},{13,14},{14,13},{17,18},{18,... | collective-permute-start | bytes 196616 | tf_op jit(solution)/shard_map/ppermute | solution.py:242
  71.4 3.5 %collective-permute-start.16 = (bf16[512,256]{1,0:T(8,128)(2,1)S(1)}, bf16[512,256]{1,0:T(8,128)(2,1)S(1)}, u32[]{:S(2)}, u32[]{:S(2)}) collective-permute-start(bf16[512,256]{1,0:T(8,128)(2,1)S(1)} %add_convert_fusion.3), channel_id=1, source_target_pairs={{1,2},{2,1},{5,6},{6,5},{9,10},{10,9},{13,14},{14,13},{17,18},{18,... | collective-permute-start | bytes 786440 | tf_op jit(solution)/shard_map/ppermute | solution.py:348
  74.9 4.1 %collective-permute-done.13 = bf16[512,256]{1,0:T(8,128)(2,1)S(1)} collective-permute-done((bf16[512,256]{1,0:T(8,128)(2,1)S(1)}, bf16[512,256]{1,0:T(8,128)(2,1)S(1)}, u32[]{:S(2)}, u32[]{:S(2)}) %collective-permute-start.13) | collective-permute-done | bytes 262176 | tf_op jit(solution)/shard_map/ppermute | solution.py:348
  81.0 3.6 %collective-permute-done.16 = bf16[512,256]{1,0:T(8,128)(2,1)S(1)} collective-permute-done((bf16[512,256]{1,0:T(8,128)(2,1)S(1)}, bf16[512,256]{1,0:T(8,128)(2,1)S(1)}, u32[]{:S(2)}, u32[]{:S(2)}) %collective-permute-start.16) | collective-permute-done | bytes 262176 | tf_op jit(solution)/shard_map/ppermute | solution.py:348
  89.1 3.5 %collective-permute-done.14 = bf16[512,256]{1,0:T(8,128)(2,1)S(1)} collective-permute-done((bf16[512,256]{1,0:T(8,128)(2,1)S(1)}, bf16[512,256]{1,0:T(8,128)(2,1)S(1)}, u32[]{:S(2)}, u32[]{:S(2)}) %collective-permute-start.14) | collective-permute-done | bytes 262176 | tf_op jit(solution)/shard_map/ppermute | solution.py:349
  92.6 4.4 %collective-permute-start.10 = (bf16[528,256]{1,0:T(8,128)(2,1)S(1)}, bf16[528,256]{1,0:T(8,128)(2,1)S(1)}, u32[]{:S(2)}, u32[]{:S(2)}) collective-permute-start(bf16[528,256]{1,0:T(8,128)(2,1)S(1)} %add_convert_fusion), channel_id=1, source_target_pairs={{1,0},{2,3},{5,4},{6,7},{9,8},{10,11},{13,12},{14,15},{17,16},{18,... | collective-permute-start | bytes 811016 | tf_op jit(solution)/shard_map/ppermute | solution.py:349
  100.9 4.4 %collective-permute-start.23 = (bf16[256,256]{1,0:T(8,128)(2,1)S(1)}, bf16[256,256]{1,0:T(8,128)(2,1)S(1)}, u32[]{:S(2)}, u32[]{:S(2)}) collective-permute-start(bf16[256,256]{1,0:T(8,128)(2,1)S(1)} %add_convert_fusion.6), channel_id=1, source_target_pairs={{1,0},{2,3},{5,4},{6,7},{9,8},{10,11},{13,12},{14,15},{17,16},{18,... | collective-permute-start | bytes 393224 | tf_op jit(solution)/shard_map/ppermute | solution.py:349
  105.4 3.3 %collective-permute-start.4 = (bf16[128,256]{1,0:T(8,128)(2,1)S(1)}, bf16[128,256]{1,0:T(8,128)(2,1)S(1)}, u32[]{:S(2)}, u32[]{:S(2)}) collective-permute-start(bf16[128,256]{1,0:T(8,128)(2,1)S(1)} %copy-done.30), channel_id=1, source_target_pairs={{8,16},{16,8},{9,17},{17,9},{10,18},{18,10},{11,19},{19,11},{12,20... | collective-permute-start | bytes 196616 | tf_op jit(solution)/shard_map/ppermute | solution.py:242
  119.6 4.3 %first_product.1.r_ref = f32[2,128,1024]{2,1,0:T(8,128)} custom-call(f32[2,128,1024]{2,1,0:T(8,128)} %get-tuple-element.29.b_ref, f32[2,128,1024]{2,1,0:T(8,128)} %couple_first.1.r_ref, s32[2]{0:T(128)} %bitcast.32, bf16[256,256]{1,0:T(8,128)(2,1)} %copy-done.4, bf16[4,256,256]{2,1,0:T(8,128)(2,1)} %get-tuple-element.36.refs_1_, bf16[512,256]{1,0:T(8,128)(2,1)} %copy-done, ...), custom_call_target="tpu_custom_call" | custom-call | flops 536870912 | bytes 4456456 | tf_op jit(solution)/shard_map/first_product/pallas_call | solution.py:42
  124.6 3.7 %first_finish.1 = (f32[2,128,1024]{2,1,0:T(8,128)}, f32[2,128,1024]{2,1,0:T(8,128)}, bf16[128,256]{1,0:T(8,128)(2,1)}, bf16[128,256]{1,0:T(8,128)(2,1)}, bf16[12...) custom-call(f32[2,128,1024]{2,1,0:T(8,128)} %get-tuple-element.29.b_ref, ...), custom_call_target="tpu_custom_call" | custom-call | flops 134217728 | bytes 2752520 | tf_op jit(solution)/shard_map/first_finish/pallas_call | solution.py:42
  130.4 3.3 %collective-permute-start.29 = (bf16[128,256]{1,0:T(8,128)(2,1)}, bf16[128,256]{1,0:T(8,128)(2,1)S(1)}, u32[]{:S(2)}, u32[]{:S(2)}) collective-permute-start(bf16[128,256]{1,0:T(8,128)(2,1)} %get-tuple-element.44), channel_id=1, source_target_pairs={{8,16},{16,8},{9,17},{17,9},{10,18},{18,10},{11,19},{19,11},{12,20... | collective-permute-start | bytes 196616 | tf_op jit(solution)/shard_map/ppermute | solution.py:242
  133.7 4.6 %second_product.1.r_ref = f32[2,128,1024]{2,1,0:T(8,128)} custom-call(f32[2,128,1024]{2,1,0:T(8,128)} %get-tuple-element.38.d_ref.d1_ref, f32[2,128,1024]{2,1,0:T(8,128)} %get-tuple-element.39.r_ref, s32[2]{0:T(128)} %bitcast.34, bf16[256,256]{1,0:T(8,128)(2,1)} %copy-done.4, bf16[4,256,256]{2,1,0:T(8,128)(2,1)} %get-tuple-element.36.refs_1_, ...), custom_call_target="tpu_custom_call" | custom-call | flops 536870912 | bytes 4718600 | tf_op jit(solution)/shard_map/second_product/pallas_call | solution.py:42
  139.7 3.6 %second_finish.1 = (f32[2,128,1024]{2,1,0:T(8,128)}, f32[2,128,1024]{2,1,0:T(8,128)}, bf16[128,256]{1,0:T(8,128)(2,1)}, bf16[128,256]{1,0:T(8,128)(2,1)}, bf16[1...) custom-call(f32[2,128,1024]{2,1,0:T(8,128)} %get-tuple-element.38.d_ref.d1_ref, ...), custom_call_target="tpu_custom_call" | custom-call | flops 100000000 | bytes 2818048 | tf_op jit(solution)/shard_map/second_finish/pallas_call | solution.py:42
  147.4 3.4 %collective-permute-start.34 = (bf16[128,256]{1,0:T(8,128)(2,1)}, bf16[128,256]{1,0:T(8,128)(2,1)S(1)}, u32[]{:S(2)}, u32[]{:S(2)}) collective-permute-start(bf16[128,256]{1,0:T(8,128)(2,1)} %get-tuple-element.52), channel_id=1, source_target_pairs={{8,16},{16,8},{9,17},{17,9},{10,18},{18,10},{11,19},{19,11},{12,20... | collective-permute-start | bytes 196616 | tf_op jit(solution)/shard_map/ppermute | solution.py:242
  150.8 5.3 %third_product.1.x_ref = f32[2,1024,128]{2,1,0:T(8,128)} custom-call(f32[2,128,1024]{2,1,0:T(8,128)} %get-tuple-element.29.b_ref, f32[2,128,1024]{2,1,0:T(8,128)} %get-tuple-element.38.d_ref.d1_ref, f32[2,128,1024]{2,1,0:T(8,128)} %get-tuple-element.45.d_ref, f32[2,128,1024]{2,1,0:T(8,128)} %get-tuple-element.46.r_ref, s32[2]{0:T(128)} %bitcast.35, ...), custom_call_target="tpu_custom_call" | custom-call | flops 536870912 | bytes 6815752 | tf_op jit(solution)/shard_map/third_product/pallas_call | solution.py:42
  (138 shorter events, 50.6 us)
Async XLA Ops:
  4.6 41.2 %collective-permute-start.5 = (bf16[256,256]{1,0:T(8,128)(2,1)}, bf16[256,256]{1,0:T(8,128)(2,1)S(1)}, u32[]{:S(2)}, u32[]{:S(2)}) collective-permute-start(bf16[256,256]{1,0:T(8,128)(2,1)} %modal_0.1), channel_id=1, source_target_pairs={{0,1},{3,2},{4,5},{7,6},{8,9},{11,10},{12,13},{15,14},{16,17},{19,... | collective-permute-start | bytes 393224 | tf_op jit(solution)/shard_map/ppermute | solution.py:347
  10.5 35.4 %collective-permute-start.21 = (bf16[256,256]{1,0:T(8,128)(2,1)}, bf16[256,256]{1,0:T(8,128)(2,1)S(1)}, u32[]{:S(2)}, u32[]{:S(2)}) collective-permute-start(bf16[256,256]{1,0:T(8,128)(2,1)} %modal_4.1), channel_id=1, source_target_pairs={{0,1},{3,2},{4,5},{7,6},{8,9},{11,10},{12,13},{15,14},{16,17},{19,... | collective-permute-start | bytes 393224 | tf_op jit(solution)/shard_map/ppermute | solution.py:347
  18.9 29.8 %collective-permute-start.12 = (bf16[512,256]{1,0:T(8,128)(2,1)}, bf16[512,256]{1,0:T(8,128)(2,1)S(1)}, u32[]{:S(2)}, u32[]{:S(2)}) collective-permute-start(bf16[512,256]{1,0:T(8,128)(2,1)} %modal_2.1), channel_id=1, source_target_pairs={{0,1},{3,2},{4,5},{7,6},{8,9},{11,10},{12,13},{15,14},{16,17},{19,... | collective-permute-start | bytes 786440 | tf_op jit(solution)/shard_map/ppermute | solution.py:347
  27.4 39.2 %collective-permute-start.15 = (bf16[512,256]{1,0:T(8,128)(2,1)}, bf16[512,256]{1,0:T(8,128)(2,1)S(1)}, u32[]{:S(2)}, u32[]{:S(2)}) collective-permute-start(bf16[512,256]{1,0:T(8,128)(2,1)} %modal_3.1), channel_id=1, source_target_pairs={{0,1},{3,2},{4,5},{7,6},{8,9},{11,10},{12,13},{15,14},{16,17},{19,... | collective-permute-start | bytes 786440 | tf_op jit(solution)/shard_map/ppermute | solution.py:347
  40.9 27.1 %collective-permute-start.8 = (bf16[528,256]{1,0:T(8,128)(2,1)}, bf16[528,256]{1,0:T(8,128)(2,1)S(1)}, u32[]{:S(2)}, u32[]{:S(2)}) collective-permute-start(bf16[528,256]{1,0:T(8,128)(2,1)} %modal_1.1), channel_id=1, source_target_pairs={{0,1},{3,2},{4,5},{7,6},{8,9},{11,10},{12,13},{15,14},{16,17},{19,... | collective-permute-start | bytes 811016 | tf_op jit(solution)/shard_map/ppermute | solution.py:347
  45.8 59.6 %collective-permute-start = (bf16[128,256]{1,0:T(8,128)(2,1)}, bf16[128,256]{1,0:T(8,128)(2,1)S(1)}, u32[]{:S(2)}, u32[]{:S(2)}) collective-permute-start(bf16[128,256]{1,0:T(8,128)(2,1)} %get-tuple-element.31), channel_id=1, source_target_pairs={{0,4},{4,0},{1,5},{5,1},{2,6},{6,2},{3,7},{7,3},{8,12},{12,8},{9,1... | collective-permute-start | bytes 196616 | tf_op jit(solution)/shard_map/ppermute | solution.py:242
  45.9 62.8 %collective-permute-start.1 = (bf16[128,256]{1,0:T(8,128)(2,1)}, bf16[128,256]{1,0:T(8,128)(2,1)S(1)}, u32[]{:S(2)}, u32[]{:S(2)}) collective-permute-start(bf16[128,256]{1,0:T(8,128)(2,1)} %get-tuple-element.32), channel_id=1, source_target_pairs={{0,1},{1,0},{2,3},{3,2},{4,5},{5,4},{6,7},{7,6},{8,9},{9,8},{10,11... | collective-permute-start | bytes 196616 | tf_op jit(solution)/shard_map/ppermute | solution.py:242
  63.1 45.8 %collective-permute-start.2 = (bf16[128,256]{1,0:T(8,128)(2,1)}, bf16[128,256]{1,0:T(8,128)(2,1)S(1)}, u32[]{:S(2)}, u32[]{:S(2)}) collective-permute-start(bf16[128,256]{1,0:T(8,128)(2,1)} %get-tuple-element.33), channel_id=1, source_target_pairs={{1,2},{2,1},{5,6},{6,5},{9,10},{10,9},{13,14},{14,13},{17,18},{18,... | collective-permute-start | bytes 196616 | tf_op jit(solution)/shard_map/ppermute | solution.py:242
  68.0 11.0 %collective-permute-start.13 = (bf16[512,256]{1,0:T(8,128)(2,1)S(1)}, bf16[512,256]{1,0:T(8,128)(2,1)S(1)}, u32[]{:S(2)}, u32[]{:S(2)}) collective-permute-start(bf16[512,256]{1,0:T(8,128)(2,1)S(1)} %add_convert_fusion.5), channel_id=1, source_target_pairs={{1,2},{2,1},{5,6},{6,5},{9,10},{10,9},{13,14},{14,13},{17,18},{18,... | collective-permute-start | bytes 786440 | tf_op jit(solution)/shard_map/ppermute | solution.py:348
  71.4 13.2 %collective-permute-start.16 = (bf16[512,256]{1,0:T(8,128)(2,1)S(1)}, bf16[512,256]{1,0:T(8,128)(2,1)S(1)}, u32[]{:S(2)}, u32[]{:S(2)}) collective-permute-start(bf16[512,256]{1,0:T(8,128)(2,1)S(1)} %add_convert_fusion.3), channel_id=1, source_target_pairs={{1,2},{2,1},{5,6},{6,5},{9,10},{10,9},{13,14},{14,13},{17,18},{18,... | collective-permute-start | bytes 786440 | tf_op jit(solution)/shard_map/ppermute | solution.py:348
  87.7 10.4 %collective-permute-start.17 = (bf16[512,256]{1,0:T(8,128)(2,1)S(1)}, bf16[512,256]{1,0:T(8,128)(2,1)S(1)}, u32[]{:S(2)}, u32[]{:S(2)}) collective-permute-start(bf16[512,256]{1,0:T(8,128)(2,1)S(1)} %add_convert_fusion.2), channel_id=1, source_target_pairs={{1,0},{2,3},{5,4},{6,7},{9,8},{10,11},{13,12},{14,15},{17,16},{18,... | collective-permute-start | bytes 786440 | tf_op jit(solution)/shard_map/ppermute | solution.py:349
  98.0 11.3 %collective-permute-start.3 = (bf16[128,256]{1,0:T(8,128)(2,1)}, bf16[128,256]{1,0:T(8,128)(2,1)S(1)}, u32[]{:S(2)}, u32[]{:S(2)}) collective-permute-start(bf16[128,256]{1,0:T(8,128)(2,1)} %get-tuple-element.34), channel_id=1, source_target_pairs={{0,8},{8,0},{16,24},{24,16},{1,9},{9,1},{17,25},{25,17},{2,10},{10... | collective-permute-start | bytes 196616 | tf_op jit(solution)/shard_map/ppermute | solution.py:242
  108.8 10.0 %collective-permute-start.18 = (bf16[256,256]{1,0:T(8,128)(2,1)S(1)}, bf16[256,256]{1,0:T(8,128)(2,1)S(1)}, u32[]{:S(2)}, u32[]{:S(2)}) collective-permute-start(bf16[256,256]{1,0:T(8,128)(2,1)S(1)} %broadcast_select_fusion.4.refs_0_), channel_id=1, source_target_pairs={{0,4},{4,0},{1,5},{5,1},{2,6},{6,2},{3,7},{7,3},{8,12},{12,8},{9,1... | collective-permute-start | bytes 393224 | tf_op jit(solution)/shard_map/ppermute | solution.py:355
  108.9 9.9 %collective-permute-start.19 = (bf16[512,256]{1,0:T(8,128)(2,1)S(1)}, bf16[512,256]{1,0:T(8,128)(2,1)S(1)}, u32[]{:S(2)}, u32[]{:S(2)}) collective-permute-start(bf16[512,256]{1,0:T(8,128)(2,1)S(1)} %broadcast_select_fusion.2.refs_2_), channel_id=1, source_target_pairs={{0,4},{4,0},{1,5},{5,1},{2,6},{6,2},{3,7},{7,3},{8,12},{12,8},{9,1... | collective-permute-start | bytes 786440 | tf_op jit(solution)/shard_map/ppermute | solution.py:355
  109.3 9.5 %collective-permute-start.20 = (bf16[512,256]{1,0:T(8,128)(2,1)S(1)}, bf16[512,256]{1,0:T(8,128)(2,1)S(1)}, u32[]{:S(2)}, u32[]{:S(2)}) collective-permute-start(bf16[512,256]{1,0:T(8,128)(2,1)S(1)} %broadcast_select_fusion.1.refs_3_), channel_id=1, source_target_pairs={{0,4},{4,0},{1,5},{5,1},{2,6},{6,2},{3,7},{7,3},{8,12},{12,8},{9,1... | collective-permute-start | bytes 786440 | tf_op jit(solution)/shard_map/ppermute | solution.py:355
  112.5 11.5 %collective-permute-start.24 = (bf16[256,256]{1,0:T(8,128)(2,1)S(1)}, bf16[256,256]{1,0:T(8,128)(2,1)S(1)}, u32[]{:S(2)}, u32[]{:S(2)}) collective-permute-start(bf16[256,256]{1,0:T(8,128)(2,1)S(1)} %broadcast_select_fusion.3.refs_0_.refs_4_), channel_id=1, source_target_pairs={{0,4},{4,0},{1,5},{5,1},{2,6},{6,2},{3,7},{7,3},{8,12},{12,8},{9,1... | collective-permute-start | bytes 393224 | tf_op jit(solution)/shard_map/ppermute | solution.py:355
  128.3 10.0 %collective-permute-start.25 = (bf16[128,256]{1,0:T(8,128)(2,1)}, bf16[128,256]{1,0:T(8,128)(2,1)S(1)}, u32[]{:S(2)}, u32[]{:S(2)}) collective-permute-start(bf16[128,256]{1,0:T(8,128)(2,1)} %get-tuple-element.40), channel_id=1, source_target_pairs={{0,4},{4,0},{1,5},{5,1},{2,6},{6,2},{3,7},{7,3},{8,12},{12,8},{9,1... | collective-permute-start | bytes 196616 | tf_op jit(solution)/shard_map/ppermute | solution.py:242
  128.3 10.0 %collective-permute-start.26 = (bf16[128,256]{1,0:T(8,128)(2,1)}, bf16[128,256]{1,0:T(8,128)(2,1)S(1)}, u32[]{:S(2)}, u32[]{:S(2)}) collective-permute-start(bf16[128,256]{1,0:T(8,128)(2,1)} %get-tuple-element.41), channel_id=1, source_target_pairs={{0,1},{1,0},{2,3},{3,2},{4,5},{5,4},{6,7},{7,6},{8,9},{9,8},{10,11... | collective-permute-start | bytes 196616 | tf_op jit(solution)/shard_map/ppermute | solution.py:242
  128.4 10.0 %collective-permute-start.27 = (bf16[128,256]{1,0:T(8,128)(2,1)}, bf16[128,256]{1,0:T(8,128)(2,1)S(1)}, u32[]{:S(2)}, u32[]{:S(2)}) collective-permute-start(bf16[128,256]{1,0:T(8,128)(2,1)} %get-tuple-element.42), channel_id=1, source_target_pairs={{1,2},{2,1},{5,6},{6,5},{9,10},{10,9},{13,14},{14,13},{17,18},{18,... | collective-permute-start | bytes 196616 | tf_op jit(solution)/shard_map/ppermute | solution.py:242
  143.3 12.8 %collective-permute-start.30 = (bf16[128,256]{1,0:T(8,128)(2,1)}, bf16[128,256]{1,0:T(8,128)(2,1)S(1)}, u32[]{:S(2)}, u32[]{:S(2)}) collective-permute-start(bf16[128,256]{1,0:T(8,128)(2,1)} %get-tuple-element.48), channel_id=1, source_target_pairs={{0,4},{4,0},{1,5},{5,1},{2,6},{6,2},{3,7},{7,3},{8,12},{12,8},{9,1... | collective-permute-start | bytes 196616 | tf_op jit(solution)/shard_map/ppermute | solution.py:242
  143.5 12.6 %collective-permute-start.31 = (bf16[128,256]{1,0:T(8,128)(2,1)}, bf16[128,256]{1,0:T(8,128)(2,1)S(1)}, u32[]{:S(2)}, u32[]{:S(2)}) collective-permute-start(bf16[128,256]{1,0:T(8,128)(2,1)} %get-tuple-element.49), channel_id=1, source_target_pairs={{0,1},{1,0},{2,3},{3,2},{4,5},{5,4},{6,7},{7,6},{8,9},{9,8},{10,11... | collective-permute-start | bytes 196616 | tf_op jit(solution)/shard_map/ppermute | solution.py:242
  144.1 12.0 %collective-permute-start.32 = (bf16[128,256]{1,0:T(8,128)(2,1)}, bf16[128,256]{1,0:T(8,128)(2,1)S(1)}, u32[]{:S(2)}, u32[]{:S(2)}) collective-permute-start(bf16[128,256]{1,0:T(8,128)(2,1)} %get-tuple-element.50), channel_id=1, source_target_pairs={{1,2},{2,1},{5,6},{6,5},{9,10},{10,9},{13,14},{14,13},{17,18},{18,... | collective-permute-start | bytes 196616 | tf_op jit(solution)/shard_map/ppermute | solution.py:242
  147.3 8.8 %collective-permute-start.33 = (bf16[128,256]{1,0:T(8,128)(2,1)}, bf16[128,256]{1,0:T(8,128)(2,1)S(1)}, u32[]{:S(2)}, u32[]{:S(2)}) collective-permute-start(bf16[128,256]{1,0:T(8,128)(2,1)} %get-tuple-element.51), channel_id=1, source_target_pairs={{0,8},{8,0},{16,24},{24,16},{1,9},{9,1},{17,25},{25,17},{2,10},{10... | collective-permute-start | bytes 196616 | tf_op jit(solution)/shard_map/ppermute | solution.py:242
  147.4 8.8 %collective-permute-start.34 = (bf16[128,256]{1,0:T(8,128)(2,1)}, bf16[128,256]{1,0:T(8,128)(2,1)S(1)}, u32[]{:S(2)}, u32[]{:S(2)}) collective-permute-start(bf16[128,256]{1,0:T(8,128)(2,1)} %get-tuple-element.52), channel_id=1, source_target_pairs={{8,16},{16,8},{9,17},{17,9},{10,18},{18,10},{11,19},{19,11},{12,20... | collective-permute-start | bytes 196616 | tf_op jit(solution)/shard_map/ppermute | solution.py:242
  (42 other events, 399.6 us)

commit v2 on v1

--- a/solution.py
+++ b/solution.py
@@ -22,6 +22,10 @@
 F32 = jnp.float32
 BF16 = jnp.bfloat16
 VMEM = pl.BlockSpec(memory_space=pltpu.VMEM)
+ANY = pl.BlockSpec(memory_space=pl.ANY)
+HBM = pl.BlockSpec(memory_space=pltpu.HBM)
+LIMIT = 12 * 2**20
+GRANT = 61 * 2**20
 SMEM = pl.BlockSpec(memory_space=pltpu.SMEM)
 
 
@@ -45,73 +49,131 @@
         in_specs=specs,
         out_specs=jax.tree.map(lambda _: VMEM, out_shape),
         cost_estimate=pl.CostEstimate(flops=flops, bytes_accessed=moved, transcendentals=0),
+        compiler_params=pltpu.CompilerParams(vmem_limit_bytes=LIMIT),
         name=name,
     )(*operands)
 
 
-def owned_boundary(bd_ref, row, count, face):
-    held = bd_ref.shape[0]
-    step = min(held, count)
+def owned_boundary(b_ref, row, height, col, width, face):
+    held = b_ref.shape[0]
+    step = min(held, height)
     parts = []
-    for start in range(row, row + count, step):
-        local = bd_ref[start % held : start % held + step, :]
+    for start in range(row, row + height, step):
+        local = b_ref[start % held : start % held + step, col : col + width]
         parts.append(jnp.where(face == start // held, local, 0.0))
     return parts[0] if len(parts) == 1 else jnp.concatenate(parts, axis=0)
 
 
-def modal_blocks(modes, stiffness, boundary, pairs, packed, name):
+def modal_blocks(modes, stiffness, boundary, chunks, after, name):
     nb, depth = modes.shape
     block = 2 * nb // SIDES
     half = block // 2
     count = nb // block
-    tile = min(1024, depth)
-    steps = depth // tile
-    rows = sorted({i for pair in pairs for i in pair})
-    lefts = sorted({i for i, _ in pairs})
-    if packed:
-        height = half * ((count + 1) // 2)
-        extra = 16 * ((2 * count + 15) // 16)
-        out_rows = 2 * height + extra
-    else:
-        out_rows = block * len(pairs)
-
-    def body(*refs):
-        k_ref = refs[0]
-        c_refs = dict(zip(rows, refs[1 : 1 + len(rows)]))
-        b_refs = refs[1 + len(rows) : 1 + len(rows) + len(pairs)]
-        out_ref, acc_ref = refs[-2:]
-        step = pl.program_id(0)
-        inverse = 1.0 / k_ref[...]
-        left = {i: (c_refs[i][...].astype(F32) * inverse).astype(BF16) for i in lefts}
-        for n, (i, j) in enumerate(pairs):
-            part = dot_nt(left[i], c_refs[j][...])
-
-            @pl.when(step == 0)
-            def _():
-                acc_ref[n] = part
-
-            @pl.when(step > 0)
-            def _():
-                acc_ref[n] += part
-
-        @pl.when(step == steps - 1)
-        def _():
-            face = lax.axis_index("face")
-            if not packed:
-                for n, (i, j) in enumerate(pairs):
-                    held = owned_boundary(b_refs[n], i * block, block, face)
-                    out_ref[n * block : (n + 1) * block, :] = (held - acc_ref[n]).astype(BF16)
-                return
+    ktile = block
+    load = min(1024, depth)
+    loads = depth // load
+    every = [pair for pairs, _ in chunks for pair in pairs]
+    rows = sorted({i for pair in every for i in pair})
+    lefts = sorted({i for i, _ in every})
+    phases = []
+    for at, (pairs, _) in enumerate(chunks):
+        if phases and sum(len(chunks[n][0]) for n in phases[-1]) + len(pairs) <= count:
+            phases[-1].append(at)
+        else:
+            phases.append([at])
+    most = max(sum(len(chunks[n][0]) for n in phase) for phase in phases)
+    height = half * ((count + 1) // 2)
+    extra = 16 * ((2 * count + 15) // 16)
+    out_shapes = [
+        shape_of((2 * height + extra if packed else block * len(pairs), block), BF16)
+        for pairs, packed in chunks
+    ]
+
+    def body(modes_ref, stiff_ref, bound_ref, *refs):
+        outs = refs[len(after) : len(after) + len(chunks)]
+        row_ref, left_ref, inverse, b_ref, sems = refs[len(after) + len(chunks) :]
+        stiff_copy = pltpu.make_async_copy(stiff_ref, inverse, sems.at[0])
+        bound_copy = pltpu.make_async_copy(bound_ref, b_ref, sems.at[1])
+        stiff_copy.start()
+        copies = {}
+        for n in range(loads):
+            cols = pl.ds(n * load, load)
+            for at, i in enumerate(rows):
+                copies[i, n] = pltpu.make_async_copy(
+                    modes_ref.at[pl.ds(i * block, block), cols],
+                    row_ref.at[at, :, cols],
+                    sems.at[2 + n * len(rows) + at],
+                )
+                copies[i, n].start()
+        bound_copy.start()
+        stiff_copy.wait()
+        inverse[...] = 1.0 / inverse[...]
+        face = lax.axis_index("face")
+        scaled_done = set()
+
+        def multiply(*accs):
+            for phase in phases:
+                pairs = [pair for n in phase for pair in chunks[n][0]]
+                columns = sorted({j for _, j in pairs})
+                for n in range(depth // ktile):
+                    cols = pl.ds(n * ktile, ktile)
+                    for i in sorted({i for pair in pairs for i in pair}):
+                        copy = copies.pop((i, n * ktile // load), None)
+                        if copy is not None:
+                            copy.wait()
+                    for i in sorted({i for i, _ in pairs}):
+                        if (i, n) not in scaled_done:
+                            scaled_done.add((i, n))
+                            value = row_ref[rows.index(i), :, cols].astype(F32)
+                            left_ref[lefts.index(i), :, cols] = (
+                                value * inverse[:, cols]
+                            ).astype(BF16)
+                    q = n % 2
+                    for at, j in enumerate(columns):
+                        register = (n // 2 * len(columns) + at) % 2
+                        pltpu.matmul_push_rhs(
+                            row_ref[rows.index(j), :, cols],
+                            staging_register=register,
+                            mxu_index=q,
+                            transpose=True,
+                        )
+                        fresh = register
+                        for m, (i, jj) in enumerate(pairs):
+                            if jj == j:
+                                pltpu.matmul_acc_lhs(
+                                    accs[2 * m + q],
+                                    left_ref[lefts.index(i), :, cols],
+                                    load_staged_rhs=fresh,
+                                )
+                                fresh = None
+                if phase[0] == 0:
+                    bound_copy.wait()
+                sums = [
+                    pltpu.matmul_pop(accs[2 * m]) + pltpu.matmul_pop(accs[2 * m + 1])
+                    for m in range(len(pairs))
+                ]
+                for n in phase:
+                    own_pairs, packed = chunks[n]
+                    write = write_packed if packed else write_plain
+                    write(outs[n], own_pairs, sums[: len(own_pairs)])
+                    sums = sums[len(own_pairs) :]
+
+        def write_plain(out_ref, pairs, sums):
+            for n, (i, j) in enumerate(pairs):
+                mine = owned_boundary(b_ref, i * block, block, j * block, block, face)
+                out_ref[n * block : (n + 1) * block, :] = (mine - sums[n]).astype(BF16)
+
+        def write_packed(out_ref, pairs, sums):
             r = lax.broadcasted_iota(jnp.int32, (half, half), 0)
             c = lax.broadcasted_iota(jnp.int32, (half, half), 1)
             rr = lax.broadcasted_iota(jnp.int32, (block, block), 0)
             cc = lax.broadcasted_iota(jnp.int32, (block, block), 1)
             highs, rests = [], []
             for n, (i, _) in enumerate(pairs):
-                held = owned_boundary(b_refs[n], i * block, block, face)
-                acc = acc_ref[n]
-                diff = held - acc
-                own = jnp.sum(jnp.where(rr == cc, held, 0.0), axis=0, keepdims=True)
+                mine = owned_boundary(b_ref, i * block, block, i * block, block, face)
+                acc = sums[n]
+                diff = mine - acc
+                own = jnp.sum(jnp.where(rr == cc, mine, 0.0), axis=0, keepdims=True)
                 modal = jnp.sum(jnp.where(rr == cc, acc, 0.0), axis=0, keepdims=True)
                 high = own.astype(BF16).astype(F32)
                 highs.append(high)
@@ -127,28 +189,30 @@
             fill = [jnp.zeros((extra - 2 * count, block), F32)] if extra > 2 * count else []
             out_ref[2 * height :, :] = jnp.concatenate(highs + rests + fill, axis=0).astype(BF16)
 
-    def row_spec(i):
-        return pl.BlockSpec((block, tile), lambda k, i=i: (i, k))
-
-    def boundary_spec(j):
-        return pl.BlockSpec((boundary.shape[0], block), lambda k, j=j: (0, j))
+        pl.run_scoped(
+            multiply, *[pltpu.ACC(q)((block, block), F32) for _ in range(most) for q in (0, 1)]
+        )
 
     return pl.pallas_call(
         body,
-        grid=(steps,),
-        out_shape=shape_of((out_rows, block), BF16),
-        in_specs=[pl.BlockSpec((1, tile), lambda k: (0, k))]
-        + [row_spec(i) for i in rows]
-        + [boundary_spec(j) for _, j in pairs],
-        out_specs=pl.BlockSpec((out_rows, block), lambda k: (0, 0)),
-        scratch_shapes=[pltpu.VMEM((len(pairs), block, block), F32)],
+        out_shape=out_shapes,
+        in_specs=[ANY] * (3 + len(after)),
+        out_specs=[VMEM] * len(chunks),
+        scratch_shapes=[
+            pltpu.VMEM((len(rows), block, depth), BF16),
+            pltpu.VMEM((len(lefts), block, depth), BF16),
+            pltpu.VMEM((1, depth), F32),
+            pltpu.VMEM(boundary.shape, F32),
+            pltpu.SemaphoreType.DMA((2 + loads * len(rows),)),
+        ],
         cost_estimate=pl.CostEstimate(
-            flops=2 * len(pairs) * block * block * depth,
+            flops=2 * len(every) * block * block * depth,
             bytes_accessed=2 * len(rows) * block * depth,
             transcendentals=0,
         ),
+        compiler_params=pltpu.CompilerParams(vmem_limit_bytes=GRANT),
         name=name,
-    )(stiffness, *([modes] * len(rows)), *([boundary] * len(pairs)))
+    )(modes, stiffness, boundary, *after)
 
 
 def unpack_diagonal(packed_list, count):
@@ -297,7 +361,58 @@
     faces = lax.axis_size("face")
     vec = (slot_total, load_count, nb)
 
-    def prepare(loads_ref, partner_ref, ports_ref, b_ref, match_ref, back_ref, *send_refs):
+    stiffness = mode_stiffness[0][None, :]
+    offs = [(i, j) for j in range(count) for i in range(j)]
+    diag = [(i, i) for i in range(count)]
+    middle = offs[1:-1]
+    plan = [(offs[:1], False)]
+    plan += [(middle[k : k + 2], False) for k in range(0, len(middle), 2)]
+    plan += [(diag, True), (offs[-1:], False)]
+    diag_at = len(plan) - 2
+
+    def add(a, b):
+        return (a.astype(F32) + b.astype(F32)).astype(BF16)
+
+    z = lax.axis_index("face")
+    inner = (z == 1) | (z == 2)
+    line = faces == 4
+
+    def tied(value, *others):
+        return lax.optimization_barrier((value, *others))[0]
+
+    def inward(part):
+        return lax.ppermute(part, "face", [(0, 1), (3, 2)])
+
+    def across(part):
+        return lax.ppermute(part, "face", [(1, 2), (2, 1)])
+
+    def outward(part):
+        return lax.ppermute(part, "face", [(1, 0), (2, 3)])
+
+    def modal(chunks, after, name):
+        return modal_blocks(modes, stiffness, boundary, chunks, after, name)
+
+    split = max(1, len(plan) - 2)
+    part = modal(plan[:1], (), "modal_0")
+    if line:
+        got = [inward(part[0])]
+    part += modal(plan[1:split], (), "modal_1")
+    if line:
+        got += [inward(p) for p in part[1:]]
+        left = [add(part[0], tied(got[0], *part[1:]))]
+        swapped = [across(left[0])]
+    part += modal(plan[split:], tuple(left) if line else (), "modal_2")
+    if line:
+        left.append(add(part[1], tied(got[1], part[-1])))
+        swapped.append(across(left[1]))
+        got += [inward(tied(p, left[1])) for p in part[split:]]
+        left.append(add(part[2], tied(got[2], left[1])))
+        swapped.append(across(left[2]))
+        total = [add(left[0], tied(swapped[0], left[2]))]
+        spread = [outward(total[0])]
+    ready = total[0] if line else part[-1]
+
+    def prepare(loads_ref, partner_ref, ports_ref, _, b_ref, match_ref, back_ref, *send_refs):
         values = []
         for s in range(slot_total):
             b = loads_ref[s].T
@@ -318,38 +433,28 @@
     bt, match, back, *sends = call(
         prepare,
         [shape_of(vec, F32), tables, tables] + send_shapes(load_count, width),
-        (rhs, partners, ports),
-        [VMEM, SMEM, VMEM],
+        (rhs, partners, ports, ready),
+        [VMEM, SMEM, VMEM, ANY],
         200_000_000,
         "prepare",
     )
 
-    stiffness = mode_stiffness[0][None, :]
-    offs = [(i, j) for j in range(count) for i in range(j)]
-    diag = [(i, i) for i in range(count)]
-    middle = offs[1:-1]
-    plan = [(offs[:1], False), (diag, True)]
-    plan += [(middle[k : k + 2], False) for k in range(0, len(middle), 2)]
-    plan += [(offs[-1:], False)]
-    partial_sums = [
-        modal_blocks(modes, stiffness, boundary, pairs, packed, f"modal_{n}")
-        for n, (pairs, packed) in enumerate(plan)
-    ]
-
-    def add(a, b):
-        return (a.astype(F32) + b.astype(F32)).astype(BF16)
-
-    def over_faces(part):
-        if faces != 4:
-            return lax.psum(part.astype(F32), "face").astype(BF16)
-        z = lax.axis_index("face")
-        inner = (z == 1) | (z == 2)
-        left = add(part, lax.ppermute(part, "face", [(0, 1), (3, 2)]))
-        total = add(left, lax.ppermute(left, "face", [(1, 2), (2, 1)]))
-        spread = lax.ppermute(total, "face", [(1, 0), (2, 3)])
-        return jnp.where(inner, total, spread)
-
-    summed = [over_faces(part) for part in partial_sums]
+    received = exchange(sends)
+
+    if line:
+        total.append(add(left[1], tied(swapped[1], *sends)))
+        spread.append(outward(total[1]))
+        for n in range(3, len(plan)):
+            left.append(add(part[n], tied(got[n], total[1], left[-1])))
+            swapped.append(across(left[n]))
+        for n in range(2, len(plan)):
+            total.append(add(left[n], tied(swapped[n], left[-1], total[-1])))
+            spread.append(outward(total[n]))
+        summed = [
+            jnp.where(inner, t, tied(s, total[-1])) for t, s in zip(total, spread)
+        ]
+    else:
+        summed = [lax.psum(p.astype(F32), "face").astype(BF16) for p in part]
 
     if insts == 2:
         candidates = [(own, lax.ppermute(own, "inst", [(0, 1), (1, 0)])) for own in summed]
@@ -364,7 +469,7 @@
                 )
             )
     options = len(candidates[0])
-    candidates[1] = tuple(unpack_diagonal(list(candidates[1]), count))
+    candidates[diag_at] = tuple(unpack_diagonal(list(candidates[diag_at]), count))
 
     def each_option(kind_ref, use):
         me = lax.axis_index("inst")
@@ -403,9 +508,8 @@
     def option_refs(refs, ids, option):
         return refs[option * len(ids) : (option + 1) * len(ids)]
 
-    received = exchange(sends)
-
-    def couple_first(b_ref, match_ref, *refs):
+
+    def couple_first(b_ref, match_ref, _, *refs):
         out_ref = refs[-1]
         values = [b_ref[s] / theta for s in range(slot_total)]
         mine = own_terms(values, port)
@@ -416,8 +520,8 @@
     r1_base = call(
         couple_first,
         shape_of(vec, F32),
-        (bt, match, *received),
-        [VMEM] * (2 + len(received)),
+        (bt, match, total[-1] if line else part[-1], *received),
+        [VMEM, VMEM, ANY] + [VMEM] * len(received),
         50_000_000,
         "couple_first",
     )

time: 161 us -> 112 us (0.70)
  Pallas kernels: 67.8 us -> 24.8 us
  local copies, waits for them, and re-layouts: 5.39 us -> 0.13 us
  other arithmetic: 1.66 us -> 3.44 us
    pallas_call x9, Pallas kernels: 32.2 us -> 10.4 us  [call(): pl.pallas_call(body, out_shape=out_shape, in_specs=specs, out_specs=jax.t...]
    pallas_call x5 -> x3, Pallas kernels: 35.5 us -> 14.4 us  [modal_blocks(): pl.pallas_call(body, out_shape=out_shapes, in_specs=[ANY] * (3 + len(afte...]
    ppermute x15, waiting for transfers between devices: 22.5 us -> 15.1 us  [the longest x5 9.07 us: outward(): return lax.ppermute(part, 'face', [(1, 0), (2, 3)])]
    ppermute x15, waiting for transfers between devices: 2.6 us -> 9.01 us  [exchange(): out.append(lax.ppermute(sends[at], axis, swaps))]
    unnamed x62 -> x16, local copies, waits for them, and re-layouts: 4.73 us -> 0.04 us
    ppermute x15, starting transfers between devices: 24 us -> 20.2 us  [exchange(): out.append(lax.ppermute(sends[at], axis, swaps))]
    ppermute x15, starting transfers between devices: 33.9 us -> 36.5 us  [the longest x5 15.4 us: across(): return lax.ppermute(part, 'face', [(1, 2), (2, 1)])]
    convert_element_type x10, other arithmetic: 1.52 us -> 3.3 us  [add(): return (a.astype(F32) + b.astype(F32)).astype(BF16)]
  transfers between devices with their start and end apart: 35 -> 35, of which waited for: 9 -> 9; matrix products, arithmetic and copies ran while one was open for 1% -> 3% of each run, Pallas kernels for 33% -> 16%
where the time goes in v2:
time: 112 us; the launch traced here: 111 us
  starting transfers between devices  57.8 us (52%)
  Pallas kernels  24.8 us (22%)
  waiting for transfers between devices  24.1 us (22%)
  other arithmetic  3.44 us (3%)
    ppermute x15, starting transfers between devices, exchange(): out.append(lax.ppermute(sends[at], axis, swaps))  20.2 us
    ppermute x5, starting transfers between devices, across(): return lax.ppermute(part, 'face', [(1, 2), (2, 1)])  15.4 us
    ppermute x5, starting transfers between devices, outward(): return lax.ppermute(part, 'face', [(1, 0), (2, 3)])  14.4 us
    pallas_call x3, Pallas kernels, modal_blocks(): pl.pallas_call(body, out_shape=out_shapes, in_specs=[ANY] * (3 + len(afte...  14.4 us
    pallas_call x9, Pallas kernels, call(): pl.pallas_call(body, out_shape=out_shape, in_specs=specs, out_specs=jax.t...  10.4 us
    ppermute x5, waiting for transfers between devices, outward(): return lax.ppermute(part, 'face', [(1, 0), (2, 3)])  9.07 us
    ppermute x15, waiting for transfers between devices, exchange(): out.append(lax.ppermute(sends[at], axis, swaps))  9.01 us
    ppermute x5, starting transfers between devices, inward(): return lax.ppermute(part, 'face', [(0, 1), (3, 2)])  6.72 us
  transfers between devices with their start and end apart: 35, of which 9 were waited for; matrix products, arithmetic and copies ran while one was open for 3% of the time, Pallas kernels for 16%

profile of v2, /device:TPU:12, one launch (start us, length us, event | category | flops | bytes accessed | tf_op | source)
XLA Modules:
  0.0 110.9 jit_solution(16234057661154907608)
XLA Ops:
  0.0 3.3 %modal_0.1 = bf16[256,256]{1,0:T(8,128)(2,1)} custom-call(bf16[1024,4096]{1,0:T(8,128)(2,1)} %bitcast.13, f32[1,4096]{1,0:T(1,128)} %stiff_ref.5, f32[256,1024]{1,0:T(8,128)} %bitcast.16), custom_call_target="tpu_custom_call" | custom-call | flops 536870912 | bytes 4194304 | tf_op jit(solution)/shard_map/modal_0/pallas_call | solution.py:196
  4.8 5.1 %modal_1.1 = (bf16[512,256]{1,0:T(8,128)(2,1)}, bf16[512,256]{1,0:T(8,128)(2,1)}) custom-call(bf16[1024,4096]{1,0:T(8,128)(2,1)} %bitcast.14, f32[1,4096]{1,0:T(1,128)} %stiff_ref.5, f32[256,1024]{1,0:T(8,128)} %bitcast.17), custom_call_target="tpu_custom_call" | custom-call | flops 2147483648 | bytes 8388608 | tf_op jit(solution)/shard_map/modal_1/pallas_call | solution.py:196
  12.9 3.5 %collective-permute-start.1 = (bf16[256,256]{1,0:T(8,128)(2,1)S(1)}, bf16[256,256]{1,0:T(8,128)(2,1)S(1)}, u32[]{:S(2)}, u32[]{:S(2)}) collective-permute-start(bf16[256,256]{1,0:T(8,128)(2,1)S(1)} %add_convert_fusion.9.refs_0_), channel_id=1, source_target_pairs={{1,2},{2,1},{5,6},{6,5},{9,10},{10,9},{13,14},{14,13},{17,18},{18,... | collective-permute-start | bytes 393224 | tf_op jit(solution)/shard_map/ppermute | solution.py:387
  16.4 5.9 %modal_2.1 = (bf16[528,256]{1,0:T(8,128)(2,1)}, bf16[256,256]{1,0:T(8,128)(2,1)}) custom-call(bf16[1024,4096]{1,0:T(8,128)(2,1)} %bitcast.15, f32[1,4096]{1,0:T(1,128)} %stiff_ref.5, f32[256,1024]{1,0:T(8,128)} %bitcast.18, bf16[256,256]{1,0:T(8,128)(2,1)} %copy-done.4), custom_call_target="tpu_custom_call" | custom-call | flops 2684354560 | bytes 8388608 | tf_op jit(solution)/shard_map/modal_2/pallas_call | solution.py:196
  22.4 2.5 %collective-permute-start.5 = (bf16[512,256]{1,0:T(8,128)(2,1)S(1)}, bf16[512,256]{1,0:T(8,128)(2,1)S(1)}, u32[]{:S(2)}, u32[]{:S(2)}) collective-permute-start(bf16[512,256]{1,0:T(8,128)(2,1)S(1)} %add_convert_fusion.5), channel_id=1, source_target_pairs={{1,2},{2,1},{5,6},{6,5},{9,10},{10,9},{13,14},{14,13},{17,18},{18,... | collective-permute-start | bytes 786440 | tf_op jit(solution)/shard_map/ppermute | solution.py:387
  26.0 3.5 %collective-permute-start.9 = (bf16[512,256]{1,0:T(8,128)(2,1)S(1)}, bf16[512,256]{1,0:T(8,128)(2,1)S(1)}, u32[]{:S(2)}, u32[]{:S(2)}) collective-permute-start(bf16[512,256]{1,0:T(8,128)(2,1)S(1)} %add_convert_fusion.4), channel_id=1, source_target_pairs={{1,2},{2,1},{5,6},{6,5},{9,10},{10,9},{13,14},{14,13},{17,18},{18,... | collective-permute-start | bytes 786440 | tf_op jit(solution)/shard_map/ppermute | solution.py:387
  31.7 4.6 %collective-permute-start.15 = (bf16[256,256]{1,0:T(8,128)(2,1)S(1)}, bf16[256,256]{1,0:T(8,128)(2,1)S(1)}, u32[]{:S(2)}, u32[]{:S(2)}) collective-permute-start(bf16[256,256]{1,0:T(8,128)(2,1)S(1)} %add_convert_fusion.8._), channel_id=1, source_target_pairs={{1,0},{2,3},{5,4},{6,7},{9,8},{10,11},{13,12},{14,15},{17,16},{18,... | collective-permute-start | bytes 393224 | tf_op jit(solution)/shard_map/ppermute | solution.py:390
  38.8 4.6 %collective-permute-start.16 = (bf16[512,256]{1,0:T(8,128)(2,1)S(1)}, bf16[512,256]{1,0:T(8,128)(2,1)S(1)}, u32[]{:S(2)}, u32[]{:S(2)}) collective-permute-start(bf16[512,256]{1,0:T(8,128)(2,1)S(1)} %add_convert_fusion.3), channel_id=1, source_target_pairs={{1,0},{2,3},{5,4},{6,7},{9,8},{10,11},{13,12},{14,15},{17,16},{18,... | collective-permute-start | bytes 786440 | tf_op jit(solution)/shard_map/ppermute | solution.py:390
  44.4 2.4 %collective-permute-start.8 = (bf16[528,256]{1,0:T(8,128)(2,1)S(1)}, bf16[528,256]{1,0:T(8,128)(2,1)S(1)}, u32[]{:S(2)}, u32[]{:S(2)}) collective-permute-start(bf16[528,256]{1,0:T(8,128)(2,1)S(1)} %add_convert_fusion.1), channel_id=1, source_target_pairs={{1,2},{2,1},{5,6},{6,5},{9,10},{10,9},{13,14},{14,13},{17,18},{18,... | collective-permute-start | bytes 811016 | tf_op jit(solution)/shard_map/ppermute | solution.py:387
  47.8 3.5 %collective-permute-start.7 = (bf16[256,256]{1,0:T(8,128)(2,1)S(1)}, bf16[256,256]{1,0:T(8,128)(2,1)S(1)}, u32[]{:S(2)}, u32[]{:S(2)}) collective-permute-start(bf16[256,256]{1,0:T(8,128)(2,1)S(1)} %add_convert_fusion.7), channel_id=1, source_target_pairs={{1,2},{2,1},{5,6},{6,5},{9,10},{10,9},{13,14},{14,13},{17,18},{18,... | collective-permute-start | bytes 393224 | tf_op jit(solution)/shard_map/ppermute | solution.py:387
  51.3 4.4 %collective-permute-done.8 = bf16[528,256]{1,0:T(8,128)(2,1)S(1)} collective-permute-done((bf16[528,256]{1,0:T(8,128)(2,1)S(1)}, bf16[528,256]{1,0:T(8,128)(2,1)S(1)}, u32[]{:S(2)}, u32[]{:S(2)}) %collective-permute-start.8) | collective-permute-done | bytes 270368 | tf_op jit(solution)/shard_map/ppermute | solution.py:387
  57.8 4.5 %collective-permute-done.17 = bf16[512,256]{1,0:T(8,128)(2,1)S(1)} collective-permute-done((bf16[512,256]{1,0:T(8,128)(2,1)S(1)}, bf16[512,256]{1,0:T(8,128)(2,1)S(1)}, u32[]{:S(2)}, u32[]{:S(2)}) %collective-permute-start.17) | collective-permute-done | bytes 262176 | tf_op jit(solution)/shard_map/ppermute | solution.py:390
  62.3 2.3 %collective-permute-start.12 = (bf16[128,256]{1,0:T(8,128)(2,1)S(1)}, bf16[128,256]{1,0:T(8,128)(2,1)S(1)}, u32[]{:S(2)}, u32[]{:S(2)}) collective-permute-start(bf16[128,256]{1,0:T(8,128)(2,1)S(1)} %get-tuple-element.62), channel_id=1, source_target_pairs={{1,2},{2,1},{5,6},{6,5},{9,10},{10,9},{13,14},{14,13},{17,18},{18,... | collective-permute-start | bytes 196616 | tf_op jit(solution)/shard_map/ppermute | solution.py:306
  64.6 2.7 %collective-permute-start.18 = (bf16[528,256]{1,0:T(8,128)(2,1)S(1)}, bf16[528,256]{1,0:T(8,128)(2,1)S(1)}, u32[]{:S(2)}, u32[]{:S(2)}) collective-permute-start(bf16[528,256]{1,0:T(8,128)(2,1)S(1)} %add_convert_fusion), channel_id=1, source_target_pairs={{1,0},{2,3},{5,4},{6,7},{9,8},{10,11},{13,12},{14,15},{17,16},{18,... | collective-permute-start | bytes 811016 | tf_op jit(solution)/shard_map/ppermute | solution.py:390
  68.8 4.6 %collective-permute-done.23 = bf16[256,256]{1,0:T(8,128)(2,1)S(1)} collective-permute-done((bf16[256,256]{1,0:T(8,128)(2,1)S(1)}, bf16[256,256]{1,0:T(8,128)(2,1)S(1)}, u32[]{:S(2)}, u32[]{:S(2)}) %collective-permute-start.23) | collective-permute-done | bytes 131104 | tf_op jit(solution)/shard_map/ppermute | solution.py:390
  74.8 2.4 %collective-permute-start.14 = (bf16[128,256]{1,0:T(8,128)(2,1)S(1)}, bf16[128,256]{1,0:T(8,128)(2,1)S(1)}, u32[]{:S(2)}, u32[]{:S(2)}) collective-permute-start(bf16[128,256]{1,0:T(8,128)(2,1)S(1)} %get-tuple-element.64), channel_id=1, source_target_pairs={{8,16},{16,8},{9,17},{17,9},{10,18},{18,10},{11,19},{19,11},{12,20... | collective-permute-start | bytes 196616 | tf_op jit(solution)/shard_map/ppermute | solution.py:306
  78.4 3.5 %collective-permute-done.14.refs_4_ = bf16[128,256]{1,0:T(8,128)(2,1)S(1)} collective-permute-done((bf16[128,256]{1,0:T(8,128)(2,1)S(1)}, bf16[128,256]{1,0:T(8,128)(2,1)S(1)}, u32[]{:S(2)}, u32[]{:S(2)}) %collective-permute-start.14) | collective-permute-done | bytes 65568 | tf_op jit(solution)/shard_map/ppermute | solution.py:306
  86.3 2.5 %collective-permute-start.26 = (bf16[128,256]{1,0:T(8,128)(2,1)S(1)}, bf16[128,256]{1,0:T(8,128)(2,1)S(1)}, u32[]{:S(2)}, u32[]{:S(2)}) collective-permute-start(bf16[128,256]{1,0:T(8,128)(2,1)S(1)} %get-tuple-element.83), channel_id=1, source_target_pairs={{0,1},{1,0},{2,3},{3,2},{4,5},{5,4},{6,7},{7,6},{8,9},{9,8},{10,11... | collective-permute-start | bytes 196616 | tf_op jit(solution)/shard_map/ppermute | solution.py:306
  88.8 2.3 %collective-permute-start.27 = (bf16[128,256]{1,0:T(8,128)(2,1)S(1)}, bf16[128,256]{1,0:T(8,128)(2,1)S(1)}, u32[]{:S(2)}, u32[]{:S(2)}) collective-permute-start(bf16[128,256]{1,0:T(8,128)(2,1)S(1)} %get-tuple-element.84), channel_id=1, source_target_pairs={{1,2},{2,1},{5,6},{6,5},{9,10},{10,9},{13,14},{14,13},{17,18},{18,... | collective-permute-start | bytes 196616 | tf_op jit(solution)/shard_map/ppermute | solution.py:306
  91.2 2.4 %collective-permute-start.29 = (bf16[128,256]{1,0:T(8,128)(2,1)S(1)}, bf16[128,256]{1,0:T(8,128)(2,1)S(1)}, u32[]{:S(2)}, u32[]{:S(2)}) collective-permute-start(bf16[128,256]{1,0:T(8,128)(2,1)S(1)} %get-tuple-element.86), channel_id=1, source_target_pairs={{8,16},{16,8},{9,17},{17,9},{10,18},{18,10},{11,19},{19,11},{12,20... | collective-permute-start | bytes 196616 | tf_op jit(solution)/shard_map/ppermute | solution.py:306
  95.5 2.8 %collective-permute-done.29.refs_4_ = bf16[128,256]{1,0:T(8,128)(2,1)S(1)} collective-permute-done((bf16[128,256]{1,0:T(8,128)(2,1)S(1)}, bf16[128,256]{1,0:T(8,128)(2,1)S(1)}, u32[]{:S(2)}, u32[]{:S(2)}) %collective-permute-start.29) | collective-permute-done | bytes 65568 | tf_op jit(solution)/shard_map/ppermute | solution.py:306
  98.9 3.5 %collective-permute-start.32 = (bf16[128,256]{1,0:T(8,128)(2,1)S(1)}, bf16[128,256]{1,0:T(8,128)(2,1)S(1)}, u32[]{:S(2)}, u32[]{:S(2)}) collective-permute-start(bf16[128,256]{1,0:T(8,128)(2,1)S(1)} %get-tuple-element.92), channel_id=1, source_target_pairs={{1,2},{2,1},{5,6},{6,5},{9,10},{10,9},{13,14},{14,13},{17,18},{18,... | collective-permute-start | bytes 196616 | tf_op jit(solution)/shard_map/ppermute | solution.py:306
  102.5 2.4 %collective-permute-start.34 = (bf16[128,256]{1,0:T(8,128)(2,1)S(1)}, bf16[128,256]{1,0:T(8,128)(2,1)S(1)}, u32[]{:S(2)}, u32[]{:S(2)}) collective-permute-start(bf16[128,256]{1,0:T(8,128)(2,1)S(1)} %get-tuple-element.94), channel_id=1, source_target_pairs={{8,16},{16,8},{9,17},{17,9},{10,18},{18,10},{11,19},{19,11},{12,20... | collective-permute-start | bytes 196616 | tf_op jit(solution)/shard_map/ppermute | solution.py:306
  107.0 2.5 %collective-permute-done.34.refs_4_ = bf16[128,256]{1,0:T(8,128)(2,1)S(1)} collective-permute-done((bf16[128,256]{1,0:T(8,128)(2,1)S(1)}, bf16[128,256]{1,0:T(8,128)(2,1)S(1)}, u32[]{:S(2)}, u32[]{:S(2)}) %collective-permute-start.34) | collective-permute-done | bytes 65568 | tf_op jit(solution)/shard_map/ppermute | solution.py:306
  (90 shorter events, 28.6 us)
Async XLA Ops:
  3.4 9.5 %collective-permute-start = (bf16[256,256]{1,0:T(8,128)(2,1)}, bf16[256,256]{1,0:T(8,128)(2,1)S(1)}, u32[]{:S(2)}, u32[]{:S(2)}) collective-permute-start(bf16[256,256]{1,0:T(8,128)(2,1)} %modal_0.1), channel_id=1, source_target_pairs={{0,1},{3,2},{4,5},{7,6},{8,9},{11,10},{12,13},{15,14},{16,17},{19,... | collective-permute-start | bytes 393224 | tf_op jit(solution)/shard_map/ppermute | solution.py:384
  10.0 12.3 %collective-permute-start.3 = (bf16[512,256]{1,0:T(8,128)(2,1)}, bf16[512,256]{1,0:T(8,128)(2,1)S(1)}, u32[]{:S(2)}, u32[]{:S(2)}) collective-permute-start(bf16[512,256]{1,0:T(8,128)(2,1)} %get-tuple-element.50), channel_id=1, source_target_pairs={{0,1},{3,2},{4,5},{7,6},{8,9},{11,10},{12,13},{15,14},{16,17},{19,... | collective-permute-start | bytes 786440 | tf_op jit(solution)/shard_map/ppermute | solution.py:384
  11.4 14.5 %collective-permute-start.2 = (bf16[512,256]{1,0:T(8,128)(2,1)}, bf16[512,256]{1,0:T(8,128)(2,1)S(1)}, u32[]{:S(2)}, u32[]{:S(2)}) collective-permute-start(bf16[512,256]{1,0:T(8,128)(2,1)} %get-tuple-element.51), channel_id=1, source_target_pairs={{0,1},{3,2},{4,5},{7,6},{8,9},{11,10},{12,13},{15,14},{16,17},{19,... | collective-permute-start | bytes 786440 | tf_op jit(solution)/shard_map/ppermute | solution.py:384
  12.9 16.6 %collective-permute-start.1 = (bf16[256,256]{1,0:T(8,128)(2,1)S(1)}, bf16[256,256]{1,0:T(8,128)(2,1)S(1)}, u32[]{:S(2)}, u32[]{:S(2)}) collective-permute-start(bf16[256,256]{1,0:T(8,128)(2,1)S(1)} %add_convert_fusion.9.refs_0_), channel_id=1, source_target_pairs={{1,2},{2,1},{5,6},{6,5},{9,10},{10,9},{13,14},{14,13},{17,18},{18,... | collective-permute-start | bytes 393224 | tf_op jit(solution)/shard_map/ppermute | solution.py:387
  22.4 16.2 %collective-permute-start.5 = (bf16[512,256]{1,0:T(8,128)(2,1)S(1)}, bf16[512,256]{1,0:T(8,128)(2,1)S(1)}, u32[]{:S(2)}, u32[]{:S(2)}) collective-permute-start(bf16[512,256]{1,0:T(8,128)(2,1)S(1)} %add_convert_fusion.5), channel_id=1, source_target_pairs={{1,2},{2,1},{5,6},{6,5},{9,10},{10,9},{13,14},{14,13},{17,18},{18,... | collective-permute-start | bytes 786440 | tf_op jit(solution)/shard_map/ppermute | solution.py:387
  26.0 21.8 %collective-permute-start.9 = (bf16[512,256]{1,0:T(8,128)(2,1)S(1)}, bf16[512,256]{1,0:T(8,128)(2,1)S(1)}, u32[]{:S(2)}, u32[]{:S(2)}) collective-permute-start(bf16[512,256]{1,0:T(8,128)(2,1)S(1)} %add_convert_fusion.4), channel_id=1, source_target_pairs={{1,2},{2,1},{5,6},{6,5},{9,10},{10,9},{13,14},{14,13},{17,18},{18,... | collective-permute-start | bytes 786440 | tf_op jit(solution)/shard_map/ppermute | solution.py:387
  29.5 9.3 %collective-permute-start.6 = (bf16[528,256]{1,0:T(8,128)(2,1)}, bf16[528,256]{1,0:T(8,128)(2,1)S(1)}, u32[]{:S(2)}, u32[]{:S(2)}) collective-permute-start(bf16[528,256]{1,0:T(8,128)(2,1)} %get-tuple-element.67), channel_id=1, source_target_pairs={{0,1},{3,2},{4,5},{7,6},{8,9},{11,10},{12,13},{15,14},{16,17},{19,... | collective-permute-start | bytes 811016 | tf_op jit(solution)/shard_map/ppermute | solution.py:384
  31.7 35.7 %collective-permute-start.15 = (bf16[256,256]{1,0:T(8,128)(2,1)S(1)}, bf16[256,256]{1,0:T(8,128)(2,1)S(1)}, u32[]{:S(2)}, u32[]{:S(2)}) collective-permute-start(bf16[256,256]{1,0:T(8,128)(2,1)S(1)} %add_convert_fusion.8._), channel_id=1, source_target_pairs={{1,0},{2,3},{5,4},{6,7},{9,8},{10,11},{13,12},{14,15},{17,16},{18,... | collective-permute-start | bytes 393224 | tf_op jit(solution)/shard_map/ppermute | solution.py:390
  36.3 8.1 %collective-permute-start.4 = (bf16[256,256]{1,0:T(8,128)(2,1)}, bf16[256,256]{1,0:T(8,128)(2,1)S(1)}, u32[]{:S(2)}, u32[]{:S(2)}) collective-permute-start(bf16[256,256]{1,0:T(8,128)(2,1)} %get-tuple-element.59), channel_id=1, source_target_pairs={{0,1},{3,2},{4,5},{7,6},{8,9},{11,10},{12,13},{15,14},{16,17},{19,... | collective-permute-start | bytes 393224 | tf_op jit(solution)/shard_map/ppermute | solution.py:384
  38.7 38.6 %collective-permute-start.10 = (bf16[128,256]{1,0:T(8,128)(2,1)S(1)}, bf16[128,256]{1,0:T(8,128)(2,1)S(1)}, u32[]{:S(2)}, u32[]{:S(2)}) collective-permute-start(bf16[128,256]{1,0:T(8,128)(2,1)S(1)} %get-tuple-element.60), channel_id=1, source_target_pairs={{0,4},{4,0},{1,5},{5,1},{2,6},{6,2},{3,7},{7,3},{8,12},{12,8},{9,1... | collective-permute-start | bytes 196616 | tf_op jit(solution)/shard_map/ppermute | solution.py:306
  38.8 25.8 %collective-permute-start.16 = (bf16[512,256]{1,0:T(8,128)(2,1)S(1)}, bf16[512,256]{1,0:T(8,128)(2,1)S(1)}, u32[]{:S(2)}, u32[]{:S(2)}) collective-permute-start(bf16[512,256]{1,0:T(8,128)(2,1)S(1)} %add_convert_fusion.3), channel_id=1, source_target_pairs={{1,0},{2,3},{5,4},{6,7},{9,8},{10,11},{13,12},{14,15},{17,16},{18,... | collective-permute-start | bytes 786440 | tf_op jit(solution)/shard_map/ppermute | solution.py:390
  44.4 11.2 %collective-permute-start.8 = (bf16[528,256]{1,0:T(8,128)(2,1)S(1)}, bf16[528,256]{1,0:T(8,128)(2,1)S(1)}, u32[]{:S(2)}, u32[]{:S(2)}) collective-permute-start(bf16[528,256]{1,0:T(8,128)(2,1)S(1)} %add_convert_fusion.1), channel_id=1, source_target_pairs={{1,2},{2,1},{5,6},{6,5},{9,10},{10,9},{13,14},{14,13},{17,18},{18,... | collective-permute-start | bytes 811016 | tf_op jit(solution)/shard_map/ppermute | solution.py:387
  47.8 10.0 %collective-permute-start.7 = (bf16[256,256]{1,0:T(8,128)(2,1)S(1)}, bf16[256,256]{1,0:T(8,128)(2,1)S(1)}, u32[]{:S(2)}, u32[]{:S(2)}) collective-permute-start(bf16[256,256]{1,0:T(8,128)(2,1)S(1)} %add_convert_fusion.7), channel_id=1, source_target_pairs={{1,2},{2,1},{5,6},{6,5},{9,10},{10,9},{13,14},{14,13},{17,18},{18,... | collective-permute-start | bytes 393224 | tf_op jit(solution)/shard_map/ppermute | solution.py:387
  57.7 19.6 %collective-permute-start.11 = (bf16[128,256]{1,0:T(8,128)(2,1)S(1)}, bf16[128,256]{1,0:T(8,128)(2,1)S(1)}, u32[]{:S(2)}, u32[]{:S(2)}) collective-permute-start(bf16[128,256]{1,0:T(8,128)(2,1)S(1)} %get-tuple-element.61), channel_id=1, source_target_pairs={{0,1},{1,0},{2,3},{3,2},{4,5},{5,4},{6,7},{7,6},{8,9},{9,8},{10,11... | collective-permute-start | bytes 196616 | tf_op jit(solution)/shard_map/ppermute | solution.py:306
  62.3 15.6 %collective-permute-start.12 = (bf16[128,256]{1,0:T(8,128)(2,1)S(1)}, bf16[128,256]{1,0:T(8,128)(2,1)S(1)}, u32[]{:S(2)}, u32[]{:S(2)}) collective-permute-start(bf16[128,256]{1,0:T(8,128)(2,1)S(1)} %get-tuple-element.62), channel_id=1, source_target_pairs={{1,2},{2,1},{5,6},{6,5},{9,10},{10,9},{13,14},{14,13},{17,18},{18,... | collective-permute-start | bytes 196616 | tf_op jit(solution)/shard_map/ppermute | solution.py:306
  64.6 10.2 %collective-permute-start.18 = (bf16[528,256]{1,0:T(8,128)(2,1)S(1)}, bf16[528,256]{1,0:T(8,128)(2,1)S(1)}, u32[]{:S(2)}, u32[]{:S(2)}) collective-permute-start(bf16[528,256]{1,0:T(8,128)(2,1)S(1)} %add_convert_fusion), channel_id=1, source_target_pairs={{1,0},{2,3},{5,4},{6,7},{9,8},{10,11},{13,12},{14,15},{17,16},{18,... | collective-permute-start | bytes 811016 | tf_op jit(solution)/shard_map/ppermute | solution.py:390
  74.8 7.0 %collective-permute-start.14 = (bf16[128,256]{1,0:T(8,128)(2,1)S(1)}, bf16[128,256]{1,0:T(8,128)(2,1)S(1)}, u32[]{:S(2)}, u32[]{:S(2)}) collective-permute-start(bf16[128,256]{1,0:T(8,128)(2,1)S(1)} %get-tuple-element.64), channel_id=1, source_target_pairs={{8,16},{16,8},{9,17},{17,9},{10,18},{18,10},{11,19},{19,11},{12,20... | collective-permute-start | bytes 196616 | tf_op jit(solution)/shard_map/ppermute | solution.py:306
  85.7 9.6 %collective-permute-start.25 = (bf16[128,256]{1,0:T(8,128)(2,1)S(1)}, bf16[128,256]{1,0:T(8,128)(2,1)S(1)}, u32[]{:S(2)}, u32[]{:S(2)}) collective-permute-start(bf16[128,256]{1,0:T(8,128)(2,1)S(1)} %get-tuple-element.82), channel_id=1, source_target_pairs={{0,4},{4,0},{1,5},{5,1},{2,6},{6,2},{3,7},{7,3},{8,12},{12,8},{9,1... | collective-permute-start | bytes 196616 | tf_op jit(solution)/shard_map/ppermute | solution.py:306
  86.3 9.0 %collective-permute-start.26 = (bf16[128,256]{1,0:T(8,128)(2,1)S(1)}, bf16[128,256]{1,0:T(8,128)(2,1)S(1)}, u32[]{:S(2)}, u32[]{:S(2)}) collective-permute-start(bf16[128,256]{1,0:T(8,128)(2,1)S(1)} %get-tuple-element.83), channel_id=1, source_target_pairs={{0,1},{1,0},{2,3},{3,2},{4,5},{5,4},{6,7},{7,6},{8,9},{9,8},{10,11... | collective-permute-start | bytes 196616 | tf_op jit(solution)/shard_map/ppermute | solution.py:306
  91.2 7.1 %collective-permute-start.29 = (bf16[128,256]{1,0:T(8,128)(2,1)S(1)}, bf16[128,256]{1,0:T(8,128)(2,1)S(1)}, u32[]{:S(2)}, u32[]{:S(2)}) collective-permute-start(bf16[128,256]{1,0:T(8,128)(2,1)S(1)} %get-tuple-element.86), channel_id=1, source_target_pairs={{8,16},{16,8},{9,17},{17,9},{10,18},{18,10},{11,19},{19,11},{12,20... | collective-permute-start | bytes 196616 | tf_op jit(solution)/shard_map/ppermute | solution.py:306
  98.8 8.2 %collective-permute-start.30 = (bf16[128,256]{1,0:T(8,128)(2,1)S(1)}, bf16[128,256]{1,0:T(8,128)(2,1)S(1)}, u32[]{:S(2)}, u32[]{:S(2)}) collective-permute-start(bf16[128,256]{1,0:T(8,128)(2,1)S(1)} %get-tuple-element.90), channel_id=1, source_target_pairs={{0,4},{4,0},{1,5},{5,1},{2,6},{6,2},{3,7},{7,3},{8,12},{12,8},{9,1... | collective-permute-start | bytes 196616 | tf_op jit(solution)/shard_map/ppermute | solution.py:306
  98.8 8.2 %collective-permute-start.31 = (bf16[128,256]{1,0:T(8,128)(2,1)S(1)}, bf16[128,256]{1,0:T(8,128)(2,1)S(1)}, u32[]{:S(2)}, u32[]{:S(2)}) collective-permute-start(bf16[128,256]{1,0:T(8,128)(2,1)S(1)} %get-tuple-element.91), channel_id=1, source_target_pairs={{0,1},{1,0},{2,3},{3,2},{4,5},{5,4},{6,7},{7,6},{8,9},{9,8},{10,11... | collective-permute-start | bytes 196616 | tf_op jit(solution)/shard_map/ppermute | solution.py:306
  98.9 8.1 %collective-permute-start.32 = (bf16[128,256]{1,0:T(8,128)(2,1)S(1)}, bf16[128,256]{1,0:T(8,128)(2,1)S(1)}, u32[]{:S(2)}, u32[]{:S(2)}) collective-permute-start(bf16[128,256]{1,0:T(8,128)(2,1)S(1)} %get-tuple-element.92), channel_id=1, source_target_pairs={{1,2},{2,1},{5,6},{6,5},{9,10},{10,9},{13,14},{14,13},{17,18},{18,... | collective-permute-start | bytes 196616 | tf_op jit(solution)/shard_map/ppermute | solution.py:306
  102.5 7.1 %collective-permute-start.34 = (bf16[128,256]{1,0:T(8,128)(2,1)S(1)}, bf16[128,256]{1,0:T(8,128)(2,1)S(1)}, u32[]{:S(2)}, u32[]{:S(2)}) collective-permute-start(bf16[128,256]{1,0:T(8,128)(2,1)S(1)} %get-tuple-element.94), channel_id=1, source_target_pairs={{8,16},{16,8},{9,17},{17,9},{10,18},{18,10},{11,19},{19,11},{12,20... | collective-permute-start | bytes 196616 | tf_op jit(solution)/shard_map/ppermute | solution.py:306
  (19 other events, 223.9 us)

commit v3 on v2

--- a/solution.py
+++ b/solution.py
@@ -64,7 +64,7 @@
     return parts[0] if len(parts) == 1 else jnp.concatenate(parts, axis=0)
 
 
-def modal_blocks(modes, stiffness, boundary, chunks, after, name):
+def modal_blocks(modes, stiffness, boundary, chunk, line, after, name):
     nb, depth = modes.shape
     block = 2 * nb // SIDES
     half = block // 2
@@ -72,26 +72,18 @@
     ktile = block
     load = min(1024, depth)
     loads = depth // load
-    every = [pair for pairs, _ in chunks for pair in pairs]
+    every = [pair for pairs, _ in chunk for pair in pairs]
     rows = sorted({i for pair in every for i in pair})
     lefts = sorted({i for i, _ in every})
-    phases = []
-    for at, (pairs, _) in enumerate(chunks):
-        if phases and sum(len(chunks[n][0]) for n in phases[-1]) + len(pairs) <= count:
-            phases[-1].append(at)
-        else:
-            phases.append([at])
-    most = max(sum(len(chunks[n][0]) for n in phase) for phase in phases)
-    height = half * ((count + 1) // 2)
+    phases = [every[k : k + count] for k in range(0, len(every), count)]
     extra = 16 * ((2 * count + 15) // 16)
-    out_shapes = [
-        shape_of((2 * height + extra if packed else block * len(pairs), block), BF16)
-        for pairs, packed in chunks
-    ]
+    tail = extra if any(packed for _, packed in chunk) else 0
+    full = max(2 if packed else len(pairs) for pairs, packed in chunk)
+    out_rows = full * block + tail
 
     def body(modes_ref, stiff_ref, bound_ref, *refs):
-        outs = refs[len(after) : len(after) + len(chunks)]
-        row_ref, left_ref, inverse, b_ref, sems = refs[len(after) + len(chunks) :]
+        keep_ref, send_ref = refs[len(after) : len(after) + 2]
+        row_ref, left_ref, inverse, b_ref, acc_ref, sems = refs[len(after) + 2 :]
         stiff_copy = pltpu.make_async_copy(stiff_ref, inverse, sems.at[0])
         bound_copy = pltpu.make_async_copy(bound_ref, b_ref, sems.at[1])
         stiff_copy.start()
@@ -112,8 +104,7 @@
         scaled_done = set()
 
         def multiply(*accs):
-            for phase in phases:
-                pairs = [pair for n in phase for pair in chunks[n][0]]
+            for p, pairs in enumerate(phases):
                 columns = sorted({j for _, j in pairs})
                 for n in range(depth // ktile):
                     cols = pl.ds(n * ktile, ktile)
@@ -146,63 +137,74 @@
                                     load_staged_rhs=fresh,
                                 )
                                 fresh = None
-                if phase[0] == 0:
-                    bound_copy.wait()
-                sums = [
-                    pltpu.matmul_pop(accs[2 * m]) + pltpu.matmul_pop(accs[2 * m + 1])
-                    for m in range(len(pairs))
+                for m in range(len(pairs)):
+                    acc_ref[p * count + m] = pltpu.matmul_pop(accs[2 * m]) + pltpu.matmul_pop(
+                        accs[2 * m + 1]
+                    )
+            bound_copy.wait()
+            base = 0
+            parts = []
+            for pairs, packed in chunk:
+                sums = [acc_ref[base + m] for m in range(len(pairs))]
+                base += len(pairs)
+                parts.append((packed_values if packed else plain_values)(pairs, sums))
+            first_kept = ((face == 0) | (face == 3)) if line else True
+            for n in range(full + (tail > 0)):
+                lines = slice(n * block, n * block + (block if n < full else tail))
+                a, b = [
+                    part[n] if n < len(part) else jnp.zeros((lines.stop - lines.start, block), F32)
+                    for part in parts
                 ]
-                for n in phase:
-                    own_pairs, packed = chunks[n]
-                    write = write_packed if packed else write_plain
-                    write(outs[n], own_pairs, sums[: len(own_pairs)])
-                    sums = sums[len(own_pairs) :]
-
-        def write_plain(out_ref, pairs, sums):
-            for n, (i, j) in enumerate(pairs):
-                mine = owned_boundary(b_ref, i * block, block, j * block, block, face)
-                out_ref[n * block : (n + 1) * block, :] = (mine - sums[n]).astype(BF16)
-
-        def write_packed(out_ref, pairs, sums):
+                keep_ref[lines, :] = jnp.where(first_kept, a, b).astype(BF16)
+                send_ref[lines, :] = jnp.where(first_kept, b, a).astype(BF16)
+
+        def plain_values(pairs, sums):
+            return [
+                owned_boundary(b_ref, i * block, block, j * block, block, face) - total
+                for (i, j), total in zip(pairs, sums)
+            ]
+
+        def packed_values(pairs, sums):
             r = lax.broadcasted_iota(jnp.int32, (half, half), 0)
             c = lax.broadcasted_iota(jnp.int32, (half, half), 1)
             rr = lax.broadcasted_iota(jnp.int32, (block, block), 0)
             cc = lax.broadcasted_iota(jnp.int32, (block, block), 1)
-            highs, rests = [], []
-            for n, (i, _) in enumerate(pairs):
+            highs, rests, both, offs = [], [], [], []
+            for (i, _), total in zip(pairs, sums):
                 mine = owned_boundary(b_ref, i * block, block, i * block, block, face)
-                acc = sums[n]
-                diff = mine - acc
+                diff = mine - total
                 own = jnp.sum(jnp.where(rr == cc, mine, 0.0), axis=0, keepdims=True)
-                modal = jnp.sum(jnp.where(rr == cc, acc, 0.0), axis=0, keepdims=True)
+                modal = jnp.sum(jnp.where(rr == cc, total, 0.0), axis=0, keepdims=True)
                 high = own.astype(BF16).astype(F32)
                 highs.append(high)
                 rests.append((own - high) - modal)
                 a = diff[:half, :half]
                 b = diff[half:, half:]
-                both = jnp.where(r < c, a, jnp.where(r > c, b, 0.0))
-                top, side = half * (n // 2), half * (n % 2)
-                out_ref[top : top + half, side : side + half] = both.astype(BF16)
-                out_ref[height + top : height + top + half, side : side + half] = diff[
-                    :half, half:
-                ].astype(BF16)
+                both.append(jnp.where(r < c, a, jnp.where(r > c, b, 0.0)))
+                offs.append(diff[:half, half:])
             fill = [jnp.zeros((extra - 2 * count, block), F32)] if extra > 2 * count else []
-            out_ref[2 * height :, :] = jnp.concatenate(highs + rests + fill, axis=0).astype(BF16)
+            return [squared(both), squared(offs), jnp.concatenate(highs + rests + fill, axis=0)]
+
+        def squared(tiles):
+            pairs = [tiles[n : n + 2] for n in range(0, len(tiles), 2)]
+            return jnp.concatenate([jnp.concatenate(two, axis=1) for two in pairs], axis=0)
 
         pl.run_scoped(
-            multiply, *[pltpu.ACC(q)((block, block), F32) for _ in range(most) for q in (0, 1)]
+            multiply,
+            *[pltpu.ACC(q)((block, block), F32) for _ in phases[0] for q in (0, 1)],
         )
 
     return pl.pallas_call(
         body,
-        out_shape=out_shapes,
+        out_shape=[shape_of((out_rows, block), BF16)] * 2,
         in_specs=[ANY] * (3 + len(after)),
-        out_specs=[VMEM] * len(chunks),
+        out_specs=[VMEM] * 2,
         scratch_shapes=[
             pltpu.VMEM((len(rows), block, depth), BF16),
             pltpu.VMEM((len(lefts), block, depth), BF16),
             pltpu.VMEM((1, depth), F32),
             pltpu.VMEM(boundary.shape, F32),
+            pltpu.VMEM((len(every), block, block), F32),
             pltpu.SemaphoreType.DMA((2 + loads * len(rows),)),
         ],
         cost_estimate=pl.CostEstimate(
@@ -215,22 +217,21 @@
     )(modes, stiffness, boundary, *after)
 
 
-def unpack_diagonal(packed_list, count):
-    block = packed_list[0].shape[1]
+def unpack_diagonal(packed_list, part, count):
+    block = packed_list[0].shape[2]
     half = block // 2
-    height = half * ((count + 1) // 2)
 
     def body(*refs):
         total = len(refs) // 2
         r = lax.broadcasted_iota(jnp.int32, (half, half), 0)
         c = lax.broadcasted_iota(jnp.int32, (half, half), 1)
         for p_ref, d_ref in zip(refs[:total], refs[total:]):
-            lines = p_ref[2 * height :, :].astype(F32)
+            lines = p_ref[part, 2 * block :, :].astype(F32)
             for i in range(count):
                 line = lines[i : i + 1, :] + lines[count + i : count + i + 1, :]
                 top, side = half * (i // 2), half * (i % 2)
-                both = p_ref[top : top + half, side : side + half].astype(F32)
-                off = p_ref[height + top : height + top + half, side : side + half]
+                both = p_ref[part, top : top + half, side : side + half].astype(F32)
+                off = p_ref[part, block + top : block + top + half, side : side + half]
                 upper = jnp.where(r < c, both, 0.0)
                 lower = jnp.where(r > c, both, 0.0)
                 a = upper + upper.T + jnp.where(r == c, line[:, :half], 0.0)
@@ -294,7 +295,7 @@
     return out
 
 
-def exchange(sends):
+def exchange(sends, skip=()):
     at = 0
     out = []
     for axis in AXES:
@@ -303,9 +304,17 @@
             swaps = []
             for p in range(first, size - 1, 2):
                 swaps += [(p, p + 1), (p + 1, p)]
-            out.append(lax.ppermute(sends[at], axis, swaps))
+            out.append(None if axis in skip else lax.ppermute(sends[at], axis, swaps))
             at += 1
     return out
+
+
+def pairings():
+    return [
+        (axis, first)
+        for axis in AXES
+        for first in ((0, 1) if lax.axis_size(axis) > 2 else (0,))
+    ]
 
 
 def send_shapes(load_count, width):
@@ -364,53 +373,47 @@
     stiffness = mode_stiffness[0][None, :]
     offs = [(i, j) for j in range(count) for i in range(j)]
     diag = [(i, i) for i in range(count)]
-    middle = offs[1:-1]
-    plan = [(offs[:1], False)]
-    plan += [(middle[k : k + 2], False) for k in range(0, len(middle), 2)]
-    plan += [(diag, True), (offs[-1:], False)]
-    diag_at = len(plan) - 2
+    tail_pairs = [(0, count - 1), (count - 2, count - 1)]
+    middle = [pair for pair in offs[2:] if pair not in tail_pairs]
+    plan = [
+        ((offs[:1], False), (offs[1:2], False)),
+        ((diag, True), (middle, False)),
+        ((tail_pairs[:1], False), (tail_pairs[1:], False)),
+    ]
 
     def add(a, b):
         return (a.astype(F32) + b.astype(F32)).astype(BF16)
 
     z = lax.axis_index("face")
-    inner = (z == 1) | (z == 2)
     line = faces == 4
+    outer = (z == 0) | (z == 3)
 
     def tied(value, *others):
         return lax.optimization_barrier((value, *others))[0]
 
-    def inward(part):
-        return lax.ppermute(part, "face", [(0, 1), (3, 2)])
+    def beside(part):
+        return lax.ppermute(part, "face", [(0, 1), (1, 0), (2, 3), (3, 2)])
 
     def across(part):
-        return lax.ppermute(part, "face", [(1, 2), (2, 1)])
-
-    def outward(part):
-        return lax.ppermute(part, "face", [(1, 0), (2, 3)])
-
-    def modal(chunks, after, name):
-        return modal_blocks(modes, stiffness, boundary, chunks, after, name)
-
-    split = max(1, len(plan) - 2)
-    part = modal(plan[:1], (), "modal_0")
+        return lax.ppermute(part, "face", [(0, 3), (3, 0), (1, 2), (2, 1)])
+
+    def modal(n, *after):
+        return modal_blocks(modes, stiffness, boundary, plan[n], line, after, f"modal_{n}")
+
+    keep_0, send_0 = modal(0)
     if line:
-        got = [inward(part[0])]
-    part += modal(plan[1:split], (), "modal_1")
+        got_0 = beside(send_0)
+    keep_1, send_1 = modal(1)
     if line:
-        got += [inward(p) for p in part[1:]]
-        left = [add(part[0], tied(got[0], *part[1:]))]
-        swapped = [across(left[0])]
-    part += modal(plan[split:], tuple(left) if line else (), "modal_2")
+        got_1 = beside(send_1)
+        left_0 = add(keep_0, tied(got_0, keep_1))
+        swap_0 = across(left_0)
+    keep_2, send_2 = modal(2, *([left_0] if line else []))
     if line:
-        left.append(add(part[1], tied(got[1], part[-1])))
-        swapped.append(across(left[1]))
-        got += [inward(tied(p, left[1])) for p in part[split:]]
-        left.append(add(part[2], tied(got[2], left[1])))
-        swapped.append(across(left[2]))
-        total = [add(left[0], tied(swapped[0], left[2]))]
-        spread = [outward(total[0])]
-    ready = total[0] if line else part[-1]
+        got_2 = beside(send_2)
+        left_1 = add(keep_1, tied(got_1, keep_2))
+        swap_1 = across(left_1)
+    ready = left_1 if line else keep_2
 
     def prepare(loads_ref, partner_ref, ports_ref, _, b_ref, match_ref, back_ref, *send_refs):
         values = []
@@ -439,22 +442,34 @@
         "prepare",
     )
 
-    received = exchange(sends)
-
     if line:
-        total.append(add(left[1], tied(swapped[1], *sends)))
-        spread.append(outward(total[1]))
-        for n in range(3, len(plan)):
-            left.append(add(part[n], tied(got[n], total[1], left[-1])))
-            swapped.append(across(left[n]))
-        for n in range(2, len(plan)):
-            total.append(add(left[n], tied(swapped[n], left[-1], total[-1])))
-            spread.append(outward(total[n]))
+        near, far = [n for n, (axis, _) in enumerate(pairings()) if axis == "face"]
+        received = exchange(sends, ("face",))
+        total_0 = add(left_0, tied(swap_0, *sends))
+        high = total_0.shape[0]
+        spread = beside(jnp.concatenate([total_0, sends[near]], axis=0))
+        spread_0, received[near] = spread[:high], spread[high:]
+        left_2 = add(keep_2, tied(got_2, total_0))
+        high = left_2.shape[0]
+        swap_2 = across(jnp.concatenate([left_2, sends[far]], axis=0))
+        total_1 = add(left_1, tied(swap_1, left_2))
+        spread_1 = beside(total_1)
+        total_2 = add(left_2, tied(swap_2[:high], total_1))
+        received[far] = swap_2[high:]
+        spread_2 = beside(total_2)
+        late = (tied(spread_0, total_2), tied(spread_1, total_2), spread_2)
         summed = [
-            jnp.where(inner, t, tied(s, total[-1])) for t, s in zip(total, spread)
+            jnp.stack([jnp.where(outer, t, s), jnp.where(outer, s, t)])
+            for t, s in zip((total_0, total_1, total_2), late)
         ]
+        after_sums = total_2
     else:
-        summed = [lax.psum(p.astype(F32), "face").astype(BF16) for p in part]
+        received = exchange(sends)
+        summed = [
+            jnp.stack([lax.psum(half.astype(F32), "face").astype(BF16) for half in halves])
+            for halves in ((keep_0, send_0), (keep_1, send_1), (keep_2, send_2))
+        ]
+        after_sums = summed[-1]
 
     if insts == 2:
         candidates = [(own, lax.ppermute(own, "inst", [(0, 1), (1, 0)])) for own in summed]
@@ -469,7 +484,7 @@
                 )
             )
     options = len(candidates[0])
-    candidates[diag_at] = tuple(unpack_diagonal(list(candidates[diag_at]), count))
+    diagonals = unpack_diagonal(list(candidates[1]), 0, count)
 
     def each_option(kind_ref, use):
         me = lax.axis_index("inst")
@@ -489,17 +504,19 @@
 
         cols = [x[:, i * block : (i + 1) * block] for i in range(count)]
         for n, ref in zip(chunk_ids, chunk_refs):
-            pairs, packed = plan[n]
-            for at, (i, j) in enumerate(pairs):
-                if packed:
+            if n == len(plan):
+                for i in range(count):
                     gather(i, dot(cols[i], ref[i]))
-                else:
-                    matrix = ref[at * block : (at + 1) * block, :]
+                continue
+            for part, (pairs, packed) in enumerate(plan[n]):
+                for at, (i, j) in enumerate([] if packed else pairs):
+                    matrix = ref[part, at * block : (at + 1) * block, :]
                     gather(j, dot(cols[i], matrix))
                     gather(i, dot_nt(cols[j], matrix))
         return acc
 
-    everything = list(range(len(plan)))
+    candidates.append(tuple(diagonals))
+    everything = [0, 1, len(plan), 2]
     flops_all = 2 * slot_total * load_count * nb * nb
 
     def matrices(ids):
@@ -520,7 +537,7 @@
     r1_base = call(
         couple_first,
         shape_of(vec, F32),
-        (bt, match, total[-1] if line else part[-1], *received),
+        (bt, match, after_sums, *received),
         [VMEM, VMEM, ANY] + [VMEM] * len(received),
         50_000_000,
         "couple_first",

time: 112 us -> 87.2 us (0.78)
  starting transfers between devices: 57.8 us -> 32.4 us
  local copies, waits for them, and re-layouts: 0.13 us -> 3.65 us
  waiting for transfers between devices: 24.1 us -> 22 us
    ppermute x30 -> x22, starting transfers between devices: 56.7 us -> 31.7 us  [the longest x13 18.1 us: exchange(): out.append(None if axis in skip else lax.ppermute(sends[at], axis, swaps))]
    slice x0 -> x4, local copies, waits for them, and re-layouts: none -> 3.52 us  [the longest x2 1.76 us: per_device(): spread_0, received[near] = (spread[:high], spread[high:])]
    ppermute x30 -> x22, waiting for transfers between devices: 24.1 us -> 22 us  [the longest x3 10.4 us: across(): return lax.ppermute(part, 'face', [(0, 3), (3, 0), (1, 2), (2, 1)])]
    convert_element_type x10 -> x6, other arithmetic: 3.3 us -> 2.09 us  [add(): return (a.astype(F32) + b.astype(F32)).astype(BF16)]
  transfers between devices with their start and end apart: 35 -> 25, of which waited for: 9 -> 8; matrix products, arithmetic and copies ran while one was open for 3% -> 8% of each run, Pallas kernels for 16% -> 20%
where the time goes in v3:
time: 87.2 us; the launch traced here: 86.9 us
  starting transfers between devices  32.4 us (37%)
  Pallas kernels  25.4 us (29%)
  waiting for transfers between devices  22 us (25%)
  local copies, waits for them, and re-layouts  3.65 us (4%)
  other arithmetic  2.99 us (3%)
    ppermute x13, starting transfers between devices, exchange(): out.append(None if axis in skip else lax.ppermute(sends[at], axis, swaps))  18.1 us
    pallas_call x3, Pallas kernels, modal_blocks(): pl.pallas_call(body, out_shape=[shape_of((out_rows, block), BF16)] * 2, i...  15.1 us
    ppermute x3, waiting for transfers between devices, across(): return lax.ppermute(part, 'face', [(0, 3), (3, 0), (1, 2), (2, 1)])  10.4 us
    pallas_call x9, Pallas kernels, call(): pl.pallas_call(body, out_shape=out_shape, in_specs=specs, out_specs=jax.t...  10.2 us
    ppermute x6, starting transfers between devices, beside(): return lax.ppermute(part, 'face', [(0, 1), (1, 0), (2, 3), (3, 2)])  7.49 us
    ppermute x13, waiting for transfers between devices, exchange(): out.append(None if axis in skip else lax.ppermute(sends[at], axis, swaps))  6.22 us
    ppermute x3, starting transfers between devices, across(): return lax.ppermute(part, 'face', [(0, 3), (3, 0), (1, 2), (2, 1)])  6.18 us
    ppermute x6, waiting for transfers between devices, beside(): return lax.ppermute(part, 'face', [(0, 1), (1, 0), (2, 3), (3, 2)])  5.38 us
  transfers between devices with their start and end apart: 25, of which 8 were waited for; matrix products, arithmetic and copies ran while one was open for 8% of the time, Pallas kernels for 20%

profile of v3, /device:TPU:12, one launch (start us, length us, event | category | flops | bytes accessed | tf_op | source)
XLA Modules:
  0.0 86.9 jit_solution(16747254858775569439)
XLA Ops:
  0.0 4.2 %modal_0.1 = (bf16[256,256]{1,0:T(8,128)(2,1)}, bf16[256,256]{1,0:T(8,128)(2,1)}) custom-call(bf16[1024,4096]{1,0:T(8,128)(2,1)} %bitcast.25, f32[1,4096]{1,0:T(1,128)} %stiff_ref.5, f32[256,1024]{1,0:T(8,128)} %bitcast.28), custom_call_target="tpu_custom_call" | custom-call | flops 1073741824 | bytes 6291456 | tf_op jit(solution)/shard_map/modal_0/pallas_call | solution.py:197
  4.7 6.7 %modal_1.1 = (bf16[528,256]{1,0:T(8,128)(2,1)}, bf16[528,256]{1,0:T(8,128)(2,1)}) custom-call(bf16[1024,4096]{1,0:T(8,128)(2,1)} %bitcast.26, f32[1,4096]{1,0:T(1,128)} %stiff_ref.5, f32[256,1024]{1,0:T(8,128)} %bitcast.29), custom_call_target="tpu_custom_call" | custom-call | flops 3221225472 | bytes 8388608 | tf_op jit(solution)/shard_map/modal_1/pallas_call | solution.py:197
  11.5 1.6 %collective-permute-start = (bf16[528,256]{1,0:T(8,128)(2,1)}, bf16[528,256]{1,0:T(8,128)(2,1)S(1)}, u32[]{:S(2)}, u32[]{:S(2)}) collective-permute-start(bf16[528,256]{1,0:T(8,128)(2,1)} %get-tuple-element.44), channel_id=1, source_target_pairs={{0,1},{1,0},{2,3},{3,2},{4,5},{5,4},{6,7},{7,6},{8,9},{9,8},{10,11... | collective-permute-start | bytes 811016 | tf_op jit(solution)/shard_map/ppermute | solution.py:395
  13.3 1.6 %collective-permute-start.3 = (bf16[256,256]{1,0:T(8,128)(2,1)S(1)}, bf16[256,256]{1,0:T(8,128)(2,1)S(1)}, u32[]{:S(2)}, u32[]{:S(2)}) collective-permute-start(bf16[256,256]{1,0:T(8,128)(2,1)S(1)} %add_convert_fusion.5.refs_0_), channel_id=1, source_target_pairs={{0,3},{3,0},{1,2},{2,1},{4,7},{7,4},{5,6},{6,5},{8,11},{11,8},{9,1... | collective-permute-start | bytes 393224 | tf_op jit(solution)/shard_map/ppermute | solution.py:398
  14.9 4.2 %modal_2.1 = (bf16[256,256]{1,0:T(8,128)(2,1)}, bf16[256,256]{1,0:T(8,128)(2,1)}) custom-call(bf16[1024,4096]{1,0:T(8,128)(2,1)} %bitcast.27, f32[1,4096]{1,0:T(1,128)} %stiff_ref.5, f32[256,1024]{1,0:T(8,128)} %bitcast.30, bf16[256,256]{1,0:T(8,128)(2,1)} %copy-done.3), custom_call_target="tpu_custom_call" | custom-call | flops 1073741824 | bytes 6291456 | tf_op jit(solution)/shard_map/modal_2/pallas_call | solution.py:197
  19.2 2.5 %collective-permute-start.2 = (bf16[256,256]{1,0:T(8,128)(2,1)}, bf16[256,256]{1,0:T(8,128)(2,1)S(1)}, u32[]{:S(2)}, u32[]{:S(2)}) collective-permute-start(bf16[256,256]{1,0:T(8,128)(2,1)} %get-tuple-element.52), channel_id=1, source_target_pairs={{0,1},{1,0},{2,3},{3,2},{4,5},{5,4},{6,7},{7,6},{8,9},{9,8},{10,11... | collective-permute-start | bytes 393224 | tf_op jit(solution)/shard_map/ppermute | solution.py:395
  21.8 2.2 %collective-permute-start.5 = (bf16[528,256]{1,0:T(8,128)(2,1)S(1)}, bf16[528,256]{1,0:T(8,128)(2,1)S(1)}, u32[]{:S(2)}, u32[]{:S(2)}) collective-permute-start(bf16[528,256]{1,0:T(8,128)(2,1)S(1)} %add_convert_fusion.1._), channel_id=1, source_target_pairs={{0,3},{3,0},{1,2},{2,1},{4,7},{7,4},{5,6},{6,5},{8,11},{11,8},{9,1... | collective-permute-start | bytes 811016 | tf_op jit(solution)/shard_map/ppermute | solution.py:398
  26.6 2.6 %collective-permute-start.7 = (bf16[384,256]{1,0:T(8,128)(2,1)S(1)}, bf16[384,256]{1,0:T(8,128)(2,1)}, u32[]{:S(2)}, u32[]{:S(2)}) collective-permute-start(bf16[384,256]{1,0:T(8,128)(2,1)S(1)} %pad_maximum_fusion.4), channel_id=1, source_target_pairs={{0,1},{1,0},{2,3},{3,2},{4,5},{5,4},{6,7},{7,6},{8,9},{9,8},{10,11... | collective-permute-start | bytes 589832 | tf_op jit(solution)/shard_map/ppermute | solution.py:395
  30.9 2.4 %collective-permute-start.4 = (bf16[384,256]{1,0:T(8,128)(2,1)}, bf16[384,256]{1,0:T(8,128)(2,1)}, u32[]{:S(2)}, u32[]{:S(2)}) collective-permute-start(bf16[384,256]{1,0:T(8,128)(2,1)} %pad_maximum_fusion.3), channel_id=1, source_target_pairs={{0,3},{3,0},{1,2},{2,1},{4,7},{7,4},{5,6},{6,5},{8,11},{11,8},{9,1... | collective-permute-start | bytes 589832 | tf_op jit(solution)/shard_map/ppermute | solution.py:398
  33.2 5.5 %collective-permute-done.5 = bf16[528,256]{1,0:T(8,128)(2,1)S(1)} collective-permute-done((bf16[528,256]{1,0:T(8,128)(2,1)S(1)}, bf16[528,256]{1,0:T(8,128)(2,1)S(1)}, u32[]{:S(2)}, u32[]{:S(2)}) %collective-permute-start.5) | collective-permute-done | bytes 270368 | tf_op jit(solution)/shard_map/ppermute | solution.py:398
  39.8 4.9 %collective-permute-done.4 = bf16[384,256]{1,0:T(8,128)(2,1)} collective-permute-done((bf16[384,256]{1,0:T(8,128)(2,1)}, bf16[384,256]{1,0:T(8,128)(2,1)}, u32[]{:S(2)}, u32[]{:S(2)}) %collective-permute-start.4) | collective-permute-done | bytes 196640 | tf_op jit(solution)/shard_map/ppermute | solution.py:398
  47.0 3.7 %collective-permute-done.13 = bf16[256,256]{1,0:T(8,128)(2,1)S(1)} collective-permute-done((bf16[256,256]{1,0:T(8,128)(2,1)S(1)}, bf16[256,256]{1,0:T(8,128)(2,1)S(1)}, u32[]{:S(2)}, u32[]{:S(2)}) %collective-permute-start.13) | collective-permute-done | bytes 131104 | tf_op jit(solution)/shard_map/ppermute | solution.py:395
  51.5 1.5 %collective-permute-start.8 = (bf16[128,256]{1,0:T(8,128)(2,1)S(1)}, bf16[128,256]{1,0:T(8,128)(2,1)S(1)}, u32[]{:S(2)}, u32[]{:S(2)}) collective-permute-start(bf16[128,256]{1,0:T(8,128)(2,1)S(1)} %get-tuple-element.56), channel_id=1, source_target_pairs={{0,8},{8,0},{16,24},{24,16},{1,9},{9,1},{17,25},{25,17},{2,10},{10... | collective-permute-start | bytes 196616 | tf_op jit(solution)/shard_map/ppermute | solution.py:307
  53.1 3.1 %collective-permute-start.9 = (bf16[128,256]{1,0:T(8,128)(2,1)S(1)}, bf16[128,256]{1,0:T(8,128)(2,1)S(1)}, u32[]{:S(2)}, u32[]{:S(2)}) collective-permute-start(bf16[128,256]{1,0:T(8,128)(2,1)S(1)} %get-tuple-element.57), channel_id=1, source_target_pairs={{8,16},{16,8},{9,17},{17,9},{10,18},{18,10},{11,19},{19,11},{12,20... | collective-permute-start | bytes 196616 | tf_op jit(solution)/shard_map/ppermute | solution.py:307
  57.9 2.2 %collective-permute-done.9.refs_4_ = bf16[128,256]{1,0:T(8,128)(2,1)S(1)} collective-permute-done((bf16[128,256]{1,0:T(8,128)(2,1)S(1)}, bf16[128,256]{1,0:T(8,128)(2,1)S(1)}, u32[]{:S(2)}, u32[]{:S(2)}) %collective-permute-start.9) | collective-permute-done | bytes 65568 | tf_op jit(solution)/shard_map/ppermute | solution.py:307
  62.2 1.6 %first_finish.1 = (f32[2,128,1024]{2,1,0:T(8,128)S(1)}, f32[2,128,1024]{2,1,0:T(8,128)S(1)}, bf16[128,256]{1,0:T(8,128)(2,1)S(1)}, bf16[128,256]{1,0:T(8,128)(2,...) custom-call(f32[2,128,1024]{2,1,0:T(8,128)S(1)} %get-tuple-element.50.b_ref, ...), custom_call_target="tpu_custom_call" | custom-call | flops 134217728 | bytes 3014664 | tf_op jit(solution)/shard_map/first_finish/pallas_call | solution.py:46
  64.8 2.2 %collective-permute-start.17 = (bf16[128,256]{1,0:T(8,128)(2,1)S(1)}, bf16[128,256]{1,0:T(8,128)(2,1)S(1)}, u32[]{:S(2)}, u32[]{:S(2)}) collective-permute-start(bf16[128,256]{1,0:T(8,128)(2,1)S(1)} %get-tuple-element.70), channel_id=1, source_target_pairs={{1,2},{2,1},{5,6},{6,5},{9,10},{10,9},{13,14},{14,13},{17,18},{18,... | collective-permute-start | bytes 196616 | tf_op jit(solution)/shard_map/ppermute | solution.py:307
  67.1 3.2 %collective-permute-start.19 = (bf16[128,256]{1,0:T(8,128)(2,1)S(1)}, bf16[128,256]{1,0:T(8,128)(2,1)S(1)}, u32[]{:S(2)}, u32[]{:S(2)}) collective-permute-start(bf16[128,256]{1,0:T(8,128)(2,1)S(1)} %get-tuple-element.72), channel_id=1, source_target_pairs={{8,16},{16,8},{9,17},{17,9},{10,18},{18,10},{11,19},{19,11},{12,20... | collective-permute-start | bytes 196616 | tf_op jit(solution)/shard_map/ppermute | solution.py:307
  70.2 1.7 %second_product.1.r_ref = f32[2,128,1024]{2,1,0:T(8,128)S(1)} custom-call(f32[2,128,1024]{2,1,0:T(8,128)S(1)} %get-tuple-element.66.d_ref.d1_ref, f32[2,128,1024]{2,1,0:T(8,128)S(1)} %get-tuple-element.67.r_ref, s32[2]{0:T(128)S(1)} %bitcast.22, bf16[2,256,256]{2,1,0:T(8,128)(2,1)S(1)} %pad_maximum_fusion.1.refs_0_, ...), custom_call_target="tpu_custom_call" | custom-call | flops 536870912 | bytes 5275656 | tf_op jit(solution)/shard_map/second_product/pallas_call | solution.py:46
  72.0 2.1 %collective-permute-done.19.refs_4_ = bf16[128,256]{1,0:T(8,128)(2,1)S(1)} collective-permute-done((bf16[128,256]{1,0:T(8,128)(2,1)S(1)}, bf16[128,256]{1,0:T(8,128)(2,1)S(1)}, u32[]{:S(2)}, u32[]{:S(2)}) %collective-permute-start.19) | collective-permute-done | bytes 65568 | tf_op jit(solution)/shard_map/ppermute | solution.py:307
  74.7 3.6 %collective-permute-start.22 = (bf16[128,256]{1,0:T(8,128)(2,1)S(1)}, bf16[128,256]{1,0:T(8,128)(2,1)S(1)}, u32[]{:S(2)}, u32[]{:S(2)}) collective-permute-start(bf16[128,256]{1,0:T(8,128)(2,1)S(1)} %get-tuple-element.78), channel_id=1, source_target_pairs={{1,2},{2,1},{5,6},{6,5},{9,10},{10,9},{13,14},{14,13},{17,18},{18,... | collective-permute-start | bytes 196616 | tf_op jit(solution)/shard_map/ppermute | solution.py:307
  78.4 3.2 %collective-permute-start.24 = (bf16[128,256]{1,0:T(8,128)(2,1)S(1)}, bf16[128,256]{1,0:T(8,128)(2,1)S(1)}, u32[]{:S(2)}, u32[]{:S(2)}) collective-permute-start(bf16[128,256]{1,0:T(8,128)(2,1)S(1)} %get-tuple-element.80), channel_id=1, source_target_pairs={{8,16},{16,8},{9,17},{17,9},{10,18},{18,10},{11,19},{19,11},{12,20... | collective-permute-start | bytes 196616 | tf_op jit(solution)/shard_map/ppermute | solution.py:307
  81.6 2.0 %third_product.1.x_ref = f32[2,1024,128]{2,1,0:T(8,128)S(1)} custom-call(f32[2,128,1024]{2,1,0:T(8,128)S(1)} %get-tuple-element.50.b_ref, f32[2,128,1024]{2,1,0:T(8,128)S(1)} %get-tuple-element.66.d_ref.d1_ref, f32[2,128,1024]{2,1,0:T(8,128)S(1)} %get-tuple-element.73.d_ref, f32[2,128,1024]{2,1,0:T(8,128)S(1)} %get-tuple-element.74.r_ref, s32[2]{0:T(128)S(1)} %bitcast.23, ...), custom_call_target="tpu_custom_call" | custom-call | flops 536870912 | bytes 7372808 | tf_op jit(solution)/shard_map/third_product/pallas_call | solution.py:46
  83.6 1.9 %collective-permute-done.24.refs_4_ = bf16[128,256]{1,0:T(8,128)(2,1)S(1)} collective-permute-done((bf16[128,256]{1,0:T(8,128)(2,1)S(1)}, bf16[128,256]{1,0:T(8,128)(2,1)S(1)}, u32[]{:S(2)}, u32[]{:S(2)}) %collective-permute-start.24) | collective-permute-done | bytes 65568 | tf_op jit(solution)/shard_map/ppermute | solution.py:307
  (70 shorter events, 15.9 us)
Async XLA Ops:
  4.2 9.0 %collective-permute-start.1 = (bf16[256,256]{1,0:T(8,128)(2,1)}, bf16[256,256]{1,0:T(8,128)(2,1)S(1)}, u32[]{:S(2)}, u32[]{:S(2)}) collective-permute-start(bf16[256,256]{1,0:T(8,128)(2,1)} %get-tuple-element.46), channel_id=1, source_target_pairs={{0,1},{1,0},{2,3},{3,2},{4,5},{5,4},{6,7},{7,6},{8,9},{9,8},{10,11... | collective-permute-start | bytes 393224 | tf_op jit(solution)/shard_map/ppermute | solution.py:395
  11.5 10.2 %collective-permute-start = (bf16[528,256]{1,0:T(8,128)(2,1)}, bf16[528,256]{1,0:T(8,128)(2,1)S(1)}, u32[]{:S(2)}, u32[]{:S(2)}) collective-permute-start(bf16[528,256]{1,0:T(8,128)(2,1)} %get-tuple-element.44), channel_id=1, source_target_pairs={{0,1},{1,0},{2,3},{3,2},{4,5},{5,4},{6,7},{7,6},{8,9},{9,8},{10,11... | collective-permute-start | bytes 811016 | tf_op jit(solution)/shard_map/ppermute | solution.py:395
  13.3 11.7 %collective-permute-start.3 = (bf16[256,256]{1,0:T(8,128)(2,1)S(1)}, bf16[256,256]{1,0:T(8,128)(2,1)S(1)}, u32[]{:S(2)}, u32[]{:S(2)}) collective-permute-start(bf16[256,256]{1,0:T(8,128)(2,1)S(1)} %add_convert_fusion.5.refs_0_), channel_id=1, source_target_pairs={{0,3},{3,0},{1,2},{2,1},{4,7},{7,4},{5,6},{6,5},{8,11},{11,8},{9,1... | collective-permute-start | bytes 393224 | tf_op jit(solution)/shard_map/ppermute | solution.py:398
  19.2 7.4 %collective-permute-start.2 = (bf16[256,256]{1,0:T(8,128)(2,1)}, bf16[256,256]{1,0:T(8,128)(2,1)S(1)}, u32[]{:S(2)}, u32[]{:S(2)}) collective-permute-start(bf16[256,256]{1,0:T(8,128)(2,1)} %get-tuple-element.52), channel_id=1, source_target_pairs={{0,1},{1,0},{2,3},{3,2},{4,5},{5,4},{6,7},{7,6},{8,9},{9,8},{10,11... | collective-permute-start | bytes 393224 | tf_op jit(solution)/shard_map/ppermute | solution.py:395
  21.8 16.9 %collective-permute-start.5 = (bf16[528,256]{1,0:T(8,128)(2,1)S(1)}, bf16[528,256]{1,0:T(8,128)(2,1)S(1)}, u32[]{:S(2)}, u32[]{:S(2)}) collective-permute-start(bf16[528,256]{1,0:T(8,128)(2,1)S(1)} %add_convert_fusion.1._), channel_id=1, source_target_pairs={{0,3},{3,0},{1,2},{2,1},{4,7},{7,4},{5,6},{6,5},{8,11},{11,8},{9,1... | collective-permute-start | bytes 811016 | tf_op jit(solution)/shard_map/ppermute | solution.py:398
  26.6 12.3 %collective-permute-start.7 = (bf16[384,256]{1,0:T(8,128)(2,1)S(1)}, bf16[384,256]{1,0:T(8,128)(2,1)}, u32[]{:S(2)}, u32[]{:S(2)}) collective-permute-start(bf16[384,256]{1,0:T(8,128)(2,1)S(1)} %pad_maximum_fusion.4), channel_id=1, source_target_pairs={{0,1},{1,0},{2,3},{3,2},{4,5},{5,4},{6,7},{7,6},{8,9},{9,8},{10,11... | collective-permute-start | bytes 589832 | tf_op jit(solution)/shard_map/ppermute | solution.py:395
  30.9 13.8 %collective-permute-start.4 = (bf16[384,256]{1,0:T(8,128)(2,1)}, bf16[384,256]{1,0:T(8,128)(2,1)}, u32[]{:S(2)}, u32[]{:S(2)}) collective-permute-start(bf16[384,256]{1,0:T(8,128)(2,1)} %pad_maximum_fusion.3), channel_id=1, source_target_pairs={{0,3},{3,0},{1,2},{2,1},{4,7},{7,4},{5,6},{6,5},{8,11},{11,8},{9,1... | collective-permute-start | bytes 589832 | tf_op jit(solution)/shard_map/ppermute | solution.py:398
  38.8 8.0 %collective-permute-start.10 = (bf16[528,256]{1,0:T(8,128)(2,1)S(1)}, bf16[528,256]{1,0:T(8,128)(2,1)S(1)}, u32[]{:S(2)}, u32[]{:S(2)}) collective-permute-start(bf16[528,256]{1,0:T(8,128)(2,1)S(1)} %add_convert_fusion), channel_id=1, source_target_pairs={{0,1},{1,0},{2,3},{3,2},{4,5},{5,4},{6,7},{7,6},{8,9},{9,8},{10,11... | collective-permute-start | bytes 811016 | tf_op jit(solution)/shard_map/ppermute | solution.py:395
  45.7 5.0 %collective-permute-start.13 = (bf16[256,256]{1,0:T(8,128)(2,1)S(1)}, bf16[256,256]{1,0:T(8,128)(2,1)S(1)}, u32[]{:S(2)}, u32[]{:S(2)}) collective-permute-start(bf16[256,256]{1,0:T(8,128)(2,1)S(1)} %add_convert_fusion.2._), channel_id=1, source_target_pairs={{0,1},{1,0},{2,3},{3,2},{4,5},{5,4},{6,7},{7,6},{8,9},{9,8},{10,11... | collective-permute-start | bytes 393224 | tf_op jit(solution)/shard_map/ppermute | solution.py:395
  46.9 13.4 %collective-permute-start.11 = (bf16[2,528,256]{2,1,0:T(8,128)(2,1)S(1)}, bf16[2,528,256]{2,1,0:T(8,128)(2,1)S(1)}, u32[]{:S(2)}, u32[]{:S(2)}) collective-permute-start(bf16[2,528,256]{2,1,0:T(8,128)(2,1)S(1)} %pad_maximum_fusion.refs_0_.refs_1_), channel_id=1, source_target_pairs={{0,4},{4,0},{1,5},{5,1},{2,6},{6,2},{3,7},{7,3},{8,12},{12,8},{9,1... | collective-permute-start | bytes 1622024 | tf_op jit(solution)/shard_map/ppermute | solution.py:475
  50.8 10.0 %collective-permute-start.12 = (bf16[2,256,256]{2,1,0:T(8,128)(2,1)S(1)}, bf16[2,256,256]{2,1,0:T(8,128)(2,1)S(1)}, u32[]{:S(2)}, u32[]{:S(2)}) collective-permute-start(bf16[2,256,256]{2,1,0:T(8,128)(2,1)S(1)} %pad_maximum_fusion.1.refs_0_), channel_id=1, source_target_pairs={{0,4},{4,0},{1,5},{5,1},{2,6},{6,2},{3,7},{7,3},{8,12},{12,8},{9,1... | collective-permute-start | bytes 786440 | tf_op jit(solution)/shard_map/ppermute | solution.py:475
  50.9 11.3 %collective-permute-start.14 = (bf16[2,256,256]{2,1,0:T(8,128)(2,1)S(1)}, bf16[2,256,256]{2,1,0:T(8,128)(2,1)S(1)}, u32[]{:S(2)}, u32[]{:S(2)}) collective-permute-start(bf16[2,256,256]{2,1,0:T(8,128)(2,1)S(1)} %pad_maximum_fusion.2.refs_0_.refs_3_), channel_id=1, source_target_pairs={{0,4},{4,0},{1,5},{5,1},{2,6},{6,2},{3,7},{7,3},{8,12},{12,8},{9,1... | collective-permute-start | bytes 786440 | tf_op jit(solution)/shard_map/ppermute | solution.py:475
  51.5 6.4 %collective-permute-start.8 = (bf16[128,256]{1,0:T(8,128)(2,1)S(1)}, bf16[128,256]{1,0:T(8,128)(2,1)S(1)}, u32[]{:S(2)}, u32[]{:S(2)}) collective-permute-start(bf16[128,256]{1,0:T(8,128)(2,1)S(1)} %get-tuple-element.56), channel_id=1, source_target_pairs={{0,8},{8,0},{16,24},{24,16},{1,9},{9,1},{17,25},{25,17},{2,10},{10... | collective-permute-start | bytes 196616 | tf_op jit(solution)/shard_map/ppermute | solution.py:307
  53.1 7.0 %collective-permute-start.9 = (bf16[128,256]{1,0:T(8,128)(2,1)S(1)}, bf16[128,256]{1,0:T(8,128)(2,1)S(1)}, u32[]{:S(2)}, u32[]{:S(2)}) collective-permute-start(bf16[128,256]{1,0:T(8,128)(2,1)S(1)} %get-tuple-element.57), channel_id=1, source_target_pairs={{8,16},{16,8},{9,17},{17,9},{10,18},{18,10},{11,19},{19,11},{12,20... | collective-permute-start | bytes 196616 | tf_op jit(solution)/shard_map/ppermute | solution.py:307
  63.9 8.1 %collective-permute-start.15 = (bf16[128,256]{1,0:T(8,128)(2,1)S(1)}, bf16[128,256]{1,0:T(8,128)(2,1)S(1)}, u32[]{:S(2)}, u32[]{:S(2)}) collective-permute-start(bf16[128,256]{1,0:T(8,128)(2,1)S(1)} %get-tuple-element.68), channel_id=1, source_target_pairs={{0,4},{4,0},{1,5},{5,1},{2,6},{6,2},{3,7},{7,3},{8,12},{12,8},{9,1... | collective-permute-start | bytes 196616 | tf_op jit(solution)/shard_map/ppermute | solution.py:307
  64.0 8.0 %collective-permute-start.16 = (bf16[128,256]{1,0:T(8,128)(2,1)S(1)}, bf16[128,256]{1,0:T(8,128)(2,1)S(1)}, u32[]{:S(2)}, u32[]{:S(2)}) collective-permute-start(bf16[128,256]{1,0:T(8,128)(2,1)S(1)} %get-tuple-element.69), channel_id=1, source_target_pairs={{0,1},{1,0},{2,3},{3,2},{4,5},{5,4},{6,7},{7,6},{8,9},{9,8},{10,11... | collective-permute-start | bytes 196616 | tf_op jit(solution)/shard_map/ppermute | solution.py:307
  64.8 7.2 %collective-permute-start.17 = (bf16[128,256]{1,0:T(8,128)(2,1)S(1)}, bf16[128,256]{1,0:T(8,128)(2,1)S(1)}, u32[]{:S(2)}, u32[]{:S(2)}) collective-permute-start(bf16[128,256]{1,0:T(8,128)(2,1)S(1)} %get-tuple-element.70), channel_id=1, source_target_pairs={{1,2},{2,1},{5,6},{6,5},{9,10},{10,9},{13,14},{14,13},{17,18},{18,... | collective-permute-start | bytes 196616 | tf_op jit(solution)/shard_map/ppermute | solution.py:307
  67.0 5.0 %collective-permute-start.18 = (bf16[128,256]{1,0:T(8,128)(2,1)S(1)}, bf16[128,256]{1,0:T(8,128)(2,1)S(1)}, u32[]{:S(2)}, u32[]{:S(2)}) collective-permute-start(bf16[128,256]{1,0:T(8,128)(2,1)S(1)} %get-tuple-element.71), channel_id=1, source_target_pairs={{0,8},{8,0},{16,24},{24,16},{1,9},{9,1},{17,25},{25,17},{2,10},{10... | collective-permute-start | bytes 196616 | tf_op jit(solution)/shard_map/ppermute | solution.py:307
  67.1 7.1 %collective-permute-start.19 = (bf16[128,256]{1,0:T(8,128)(2,1)S(1)}, bf16[128,256]{1,0:T(8,128)(2,1)S(1)}, u32[]{:S(2)}, u32[]{:S(2)}) collective-permute-start(bf16[128,256]{1,0:T(8,128)(2,1)S(1)} %get-tuple-element.72), channel_id=1, source_target_pairs={{8,16},{16,8},{9,17},{17,9},{10,18},{18,10},{11,19},{19,11},{12,20... | collective-permute-start | bytes 196616 | tf_op jit(solution)/shard_map/ppermute | solution.py:307
  74.6 9.0 %collective-permute-start.20 = (bf16[128,256]{1,0:T(8,128)(2,1)S(1)}, bf16[128,256]{1,0:T(8,128)(2,1)S(1)}, u32[]{:S(2)}, u32[]{:S(2)}) collective-permute-start(bf16[128,256]{1,0:T(8,128)(2,1)S(1)} %get-tuple-element.76), channel_id=1, source_target_pairs={{0,4},{4,0},{1,5},{5,1},{2,6},{6,2},{3,7},{7,3},{8,12},{12,8},{9,1... | collective-permute-start | bytes 196616 | tf_op jit(solution)/shard_map/ppermute | solution.py:307
  74.6 9.0 %collective-permute-start.21 = (bf16[128,256]{1,0:T(8,128)(2,1)S(1)}, bf16[128,256]{1,0:T(8,128)(2,1)S(1)}, u32[]{:S(2)}, u32[]{:S(2)}) collective-permute-start(bf16[128,256]{1,0:T(8,128)(2,1)S(1)} %get-tuple-element.77), channel_id=1, source_target_pairs={{0,1},{1,0},{2,3},{3,2},{4,5},{5,4},{6,7},{7,6},{8,9},{9,8},{10,11... | collective-permute-start | bytes 196616 | tf_op jit(solution)/shard_map/ppermute | solution.py:307
  74.7 8.9 %collective-permute-start.22 = (bf16[128,256]{1,0:T(8,128)(2,1)S(1)}, bf16[128,256]{1,0:T(8,128)(2,1)S(1)}, u32[]{:S(2)}, u32[]{:S(2)}) collective-permute-start(bf16[128,256]{1,0:T(8,128)(2,1)S(1)} %get-tuple-element.78), channel_id=1, source_target_pairs={{1,2},{2,1},{5,6},{6,5},{9,10},{10,9},{13,14},{14,13},{17,18},{18,... | collective-permute-start | bytes 196616 | tf_op jit(solution)/shard_map/ppermute | solution.py:307
  78.4 5.3 %collective-permute-start.23 = (bf16[128,256]{1,0:T(8,128)(2,1)S(1)}, bf16[128,256]{1,0:T(8,128)(2,1)S(1)}, u32[]{:S(2)}, u32[]{:S(2)}) collective-permute-start(bf16[128,256]{1,0:T(8,128)(2,1)S(1)} %get-tuple-element.79), channel_id=1, source_target_pairs={{0,8},{8,0},{16,24},{24,16},{1,9},{9,1},{17,25},{25,17},{2,10},{10... | collective-permute-start | bytes 196616 | tf_op jit(solution)/shard_map/ppermute | solution.py:307
  78.4 7.1 %collective-permute-start.24 = (bf16[128,256]{1,0:T(8,128)(2,1)S(1)}, bf16[128,256]{1,0:T(8,128)(2,1)S(1)}, u32[]{:S(2)}, u32[]{:S(2)}) collective-permute-start(bf16[128,256]{1,0:T(8,128)(2,1)S(1)} %get-tuple-element.80), channel_id=1, source_target_pairs={{8,16},{16,8},{9,17},{17,9},{10,18},{18,10},{11,19},{19,11},{12,20... | collective-permute-start | bytes 196616 | tf_op jit(solution)/shard_map/ppermute | solution.py:307
  (8 other events, 116.8 us)
